TPU v7x, 16 devices: a whole 2x2x2 slice. The times are simulated.
16 devices in a mesh: dp: 4 (over z, y), dcp: 4 (over x, core).
Axes of the slice: x: 2, y: 2, z: 2, core: 2. Of those that a mesh axis runs over, the one named last changes fastest.
Arguments:
- q_abs: bfloat16 [128, 64, 576], P('dp', 'dcp'), parts along dimension 0
- cache: bfloat16 [128, 8192, 576], P('dp', 'dcp'), parts along dimension 0
- lengths: int32 [128], P('dp'), parts along dimension 0
Outputs:
- output: bfloat16 [128, 64, 512], P('dp', 'dcp'), parts along dimension 0
There are 4 independent parts. A program takes and returns all parts, laid end to end along the dimension named above; each array names one.
All inputs are finite; a program needn't handle non-finite values.
Results may differ from a plain program's by a relative error of at most 0.00673794.
Values are sent between devices in bfloat16 or wider.
A program may use at most 1 GiB of HBM per device.

v0:
```python
import jax
import jax.numpy as jnp
from jax import lax
from jax.sharding import PartitionSpec as P

ROPE = 64
SCALE = 192 ** -0.5


def partial_attention(q, blk, valid, lat):
    s = jnp.einsum('bhk,btk->bht', q, blk, preferred_element_type=jnp.float32) * SCALE
    s = jnp.where(valid[:, None, :], s, -jnp.inf)
    m = jnp.max(s, axis=2)
    m0 = jnp.where(jnp.isfinite(m), m, 0.0)
    p = jnp.exp(s - m0[:, :, None])
    l = jnp.sum(p, axis=2)
    pv = jnp.einsum('bht,btc->bhc', p.astype(jnp.bfloat16), blk[:, :, :lat], preferred_element_type=jnp.float32)
    has = l > 0.0
    l1 = jnp.where(has, l, 1.0)
    od = (pv / l1[:, :, None]).astype(jnp.bfloat16)
    lse = jnp.where(has, m0 + jnp.log(l1), -jnp.inf)
    return od, lse


def merge(od, lse, axis):
    mx = jnp.max(lse, axis=axis, keepdims=True)
    wt = jnp.exp(lse - mx)
    wt = wt / jnp.sum(wt, axis=axis, keepdims=True)
    return jnp.sum(wt[..., None] * od.astype(jnp.float32), axis=axis).astype(jnp.bfloat16)


def solution(mesh):
    n = mesh.shape['dcp']

    def local(q, cache, lengths):
        d = lax.axis_index('dcp')
        b, sl, wd = cache.shape
        lat = wd - ROPE
        qa = lax.all_gather(q, 'dcp', axis=1, tiled=True)
        pos = d * sl + jnp.arange(sl)
        valid = pos[None, :] < lengths[:, None]
        od, lse = partial_attention(qa, cache, valid, lat)
        h = od.shape[1]
        od = od.reshape(b, n, h // n, lat)
        lse = lse.reshape(b, n, h // n)
        od = lax.all_to_all(od, 'dcp', 1, 1, tiled=True)
        lse = lax.all_to_all(lse, 'dcp', 1, 1, tiled=True)
        return merge(od, lse, 1)

    return jax.shard_map(local, mesh=mesh, in_specs=(P('dp', 'dcp', None), P('dp', 'dcp', None), P('dp')), out_specs=P('dp', 'dcp', None), check_vma=False)
```

profile of v0, /device:TPU:0, one launch (start us, length us, event | category | flops | bytes accessed | tf_op | source)
XLA Modules:
  0.0 151.6 jit_solution(2083109895700252910)
XLA Ops:
  6.5 0.0 all-gather.2.cloned.1.call-start
  6.5 0.7 all-gather.2.cloned.1.call-update
  7.3 0.8 broadcast_compare_fusion
  8.0 27.0 %all-gather.2.cloned.1.call-done = bf16[32,64,576]{2,1,0:T(8,128)(2,1)} async-done(((bf16[32,16,576]{2,1,0:T(8,128)(2,1)}), bf16[32,64,576]{2,1,0:T(8,128)(2,1)}) %all-gather.2.cloned.1.call-update) | async-done | bytes 2359312 | tf_op jit(solution)/shard_map/all_gather | solution.py:39
  35.1 33.4 %fusion.2 = (f32[32,64]{1,0:T(8,128)S(1)}, f32[32,64,2048]{2,1,0:T(8,128)}) fusion(pred[32,2048]{1,0:T(8,128)(4,1)S(1)} %broadcast_compare_fusion, bf16[32,64,576]{2,1,0:T(8,128)(2,1)} %all-gather.2.cloned.1.call-done, bf16[32,2048,576]{1,2,0:T(8,128)(2,1)} %param.4), kind=kOutput, calls=%fused_computation.4 | convolution fusion | flops 4844419072 | bytes 94707712 | tf_op jit(solution)/shard_map/bhk,btk->bht/dot_general | solution.py:11
  68.5 0.1 copy.10
  68.5 8.0 %fusion.4 = f32[32,64]{1,0:T(8,128)S(1)} fusion(f32[32,64,2048]{2,1,0:T(8,128)} %get-tuple-element.6, f32[32,64]{1,0:T(8,128)S(1)} %is-finite_select_fusion.1, pred[32,2048]{1,0:T(8,128)(4,1)S(1)} %broadcast_compare_fusion), kind=kLoop, calls=%fused_computation.6 | loop fusion | flops 16775168 | bytes 16859136 | tf_op jit(solution)/shard_map/reduce_sum | solution.py:16
  76.6 0.1 copy.9
  76.7 0.7 reshape.45
  77.4 3.2 %all-to-all-start = ((f32[4,1,512]{2,1,0:T(1,128)}), f32[4,1,512]{2,1,0:T(1,128)S(1)}, u32[]{:S(2)}, u32[]{:S(2)}) async-start(f32[4,1,512]{2,1,0:T(1,128)} %reshape.45), calls=%async_computation | async-start | bytes 16384 | tf_op jit(solution)/shard_map/all_to_all | solution.py:47
  80.6 32.3 %divide_convert_fusion = bf16[32,64,512]{2,1,0:T(8,128)(2,1)S(1)} fusion(bf16[32,2048,576]{1,2,0:T(8,128)(2,1)} %param.4, f32[32,64,2048]{2,1,0:T(8,128)} %get-tuple-element.6, f32[32,64]{1,0:T(8,128)S(1)} %is-finite_select_fusion.1, pred[32,2048]{1,0:T(8,128)(4,1)S(1)} %broadcast_compare_fusion, f32[32,64]{1,0:T(8,128)S(1)} %compare_select_fusion), kind=kOutput, calls=%fused_computation.12 | convolution fusion | flops 4313841664 | bytes 86065152 | tf_op jit(solution)/shard_map/bht,btc->bhc/dot_general | solution.py:17
  112.9 1.6 %copy.13 = bf16[32,4,16,512]{3,2,0,1:T(8,128)(2,1)} copy(bf16[32,4,16,512]{3,2,1,0:T(8,128)(2,1)S(1)} %bitcast.11) | data formatting | bytes 4194304 | tf_op jit(solution)/shard_map/reshape | solution.py:44
  114.5 0.0 all-to-all-done
  114.5 3.6 %all-to-all-start.1 = ((bf16[32,4,16,512]{3,2,0,1:T(8,128)(2,1)}), bf16[32,4,16,512]{3,2,0,1:T(8,128)(2,1)S(1)}, u32[]{:S(2)}, u32[]{:S(2)}) async-start(bf16[32,4,16,512]{3,2,0,1:T(8,128)(2,1)} %copy.13), calls=%async_computation.1 | async-start | bytes 4194304 | tf_op jit(solution)/shard_map/all_to_all | solution.py:46
  118.1 0.5 broadcast.38
  118.6 0.7 reduce
  119.3 0.1 reshape.46
  119.4 0.1 copy.11
  119.5 24.0 %all-to-all-done.1 = bf16[32,4,16,512]{3,2,0,1:T(8,128)(2,1)S(1)} async-done(((bf16[32,4,16,512]{3,2,0,1:T(8,128)(2,1)}), bf16[32,4,16,512]{3,2,0,1:T(8,128)(2,1)S(1)}, u32[]{:S(2)}, u32[]{:S(2)}) %all-to-all-start.1) | async-done | bytes 2097184 | tf_op jit(solution)/shard_map/all_to_all | solution.py:46
  143.5 1.3 multiply_reduce_fusion
  (7 shorter events, 0.1 us)
Async XLA Ops:
  6.5 28.5 %all-gather.2.cloned.1.call-start = ((), (), s32[]{:S(2)}) async-start(), calls=%async_computation.2 | async-start | bytes 3276800 | tf_op jit(solution)/shard_map/all_gather | solution.py:39
  77.4 37.1 %all-to-all-start = ((f32[4,1,512]{2,1,0:T(1,128)}), f32[4,1,512]{2,1,0:T(1,128)S(1)}, u32[]{:S(2)}, u32[]{:S(2)}) async-start(f32[4,1,512]{2,1,0:T(1,128)} %reshape.45), calls=%async_computation | async-start | bytes 16384 | tf_op jit(solution)/shard_map/all_to_all | solution.py:47
  114.5 29.0 %all-to-all-start.1 = ((bf16[32,4,16,512]{3,2,0,1:T(8,128)(2,1)}), bf16[32,4,16,512]{3,2,0,1:T(8,128)(2,1)S(1)}, u32[]{:S(2)}, u32[]{:S(2)}) async-start(bf16[32,4,16,512]{3,2,0,1:T(8,128)(2,1)} %copy.13), calls=%async_computation.1 | async-start | bytes 4194304 | tf_op jit(solution)/shard_map/all_to_all | solution.py:46
Sparse Core Ops, SparseCore 0:
  8.9 26.1 all-gather.1
where the time goes:
time: 152 us
  matrix products  65.7 us (43%)
  waiting for transfers between devices  51.8 us (34%)
  between operations  13.5 us (9%)
  other arithmetic  10.8 us (7%)
  starting transfers between devices  6.86 us (5%)
  local copies, waits for them, and re-layouts  3.09 us (2%)
    dot_general x1, matrix products, partial_attention(): jnp.einsum('bhk,btk->bht', q, blk, preferred_element_type=jnp.float32)  33.4 us
    dot_general x1, matrix products, partial_attention(): jnp.einsum('bht,btc->bhc', p.astype(jnp.bfloat16), blk[:, :, :lat], prefe...  32.3 us
    all_gather x1, waiting for transfers between devices, local(): qa = lax.all_gather(q, 'dcp', axis=1, tiled=True)  27 us
    all_to_all x1, waiting for transfers between devices, local(): od = lax.all_to_all(od, 'dcp', 1, 1, tiled=True)  24 us
    reduce_sum x1, other arithmetic, partial_attention(): l = jnp.sum(p, axis=2)  8.02 us
    all_to_all x1, starting transfers between devices, local(): od = lax.all_to_all(od, 'dcp', 1, 1, tiled=True)  3.61 us
    all_to_all x1, starting transfers between devices, local(): lse = lax.all_to_all(lse, 'dcp', 1, 1, tiled=True)  3.25 us
  transfers between devices with their start and end apart: 3, of which 2 were waited for; matrix products, arithmetic and copies ran while one was open for 24% of the time, Pallas kernels for 0%

commit v1 on v0

v1 whole, which is shorter than its diff:
```python
import functools

import jax
import jax.numpy as jnp
from jax import lax
from jax.experimental import pallas as pl
from jax.experimental.pallas import tpu as pltpu
from jax.sharding import PartitionSpec as P

ROPE = 64
SCALE = 192 ** -0.5
LOG2E = 1.4426950408889634
SLOTS = 8


def kernel(len_ref, q_ref, cache_ref, out_ref, cbuf, qbuf, s_a, s_b, mx_a, mx_b, obuf, orecv, lbuf, lrecv,
           c_sem, q_sem, qs_sem, qr_sem, os_sem, or_sem, ls_sem, lr_sem):
    nb, heads, wd = qbuf.shape
    own = q_ref.shape[1]
    lat = wd - ROPE
    sl = cbuf.shape[2]
    pairs = nb // 2
    g = lax.axis_index('dp')
    d = lax.axis_index('dcp')
    mate = d + 1 - 2 * (d % 2)
    over = (d + 2) % 4
    far = mate + 2 - 4 * (mate // 2)
    peers = (mate, over, far)

    def rows(j):
        return pl.ds(pl.multiple_of(j * own, own), own)

    def cache_copy(b):
        slot = b % SLOTS
        return pltpu.make_async_copy(cache_ref.at[b], cbuf.at[slot], c_sem.at[slot])

    def remote(src, dst, ssem, rsem, dev):
        return pltpu.make_async_remote_copy(src_ref=src, dst_ref=dst, send_sem=ssem, recv_sem=rsem,
                                            device_id=(g, dev), device_id_type=pl.DeviceIdType.MESH)

    def q_copy(kind, c, src_dev, to):
        view = qbuf.at[pl.ds(2 * c, 2), rows(src_dev), :]
        return remote(view, view, qs_sem.at[kind, c], qr_sem.at[kind, c], to)

    def o_copy(i, b, src_dev, dst_dev):
        return remote(obuf.at[b, rows(dst_dev), :], orecv.at[src_dev, b], os_sem.at[i, b], or_sem.at[i, b], dst_dev)

    def l_copy(i, src_dev, dst_dev):
        return remote(lbuf.at[rows(dst_dev), :], lrecv.at[src_dev], ls_sem.at[i], lr_sem.at[i], dst_dev)

    q_own = pltpu.make_async_copy(q_ref, qbuf.at[:, rows(d), :], q_sem)
    q_own.start()
    for b in range(6):
        cache_copy(b).start()

    barrier = pltpu.get_barrier_semaphore()
    for p in peers:
        pl.semaphore_signal(barrier, inc=1, device_id=(g, p), device_id_type=pl.DeviceIdType.MESH)
    pl.semaphore_wait(barrier, 3)

    q_own.wait()

    def send_q(c, _):
        q_copy(1, c, d, over).start()
        q_copy(0, c, d, mate).start()
        return 0

    lax.fori_loop(0, pairs, send_q, 0)

    def forward_q(c):
        q_copy(1, c, over, over).wait_recv()
        q_copy(2, c, over, mate).start()

    def wait_q(c):
        q_copy(0, c, mate, mate).wait_recv()
        q_copy(2, c, far, mate).wait_recv()

    def send_o(b):
        for i in (1, 2, 0):
            o_copy(i, b, d, peers[i]).start()

    def scores(b, s_ref, mx_ref):
        n_valid = len_ref[b] - d * sl
        c = cbuf.at[b % SLOTS]
        s = jnp.dot(qbuf[b], c[...], preferred_element_type=jnp.float32)
        pos = lax.broadcasted_iota(jnp.int32, s.shape, 1)
        s = jnp.where(pos < n_valid, s, -jnp.inf)
        s_ref[...] = s
        mx = s[:, :128]
        for k in range(1, sl // 128):
            mx = jnp.maximum(mx, s[:, 128 * k:128 * (k + 1)])
        mx_ref[...] = mx

    def values(b, s_ref, mx_ref):
        c = cbuf.at[b % SLOTS]
        m = jnp.max(mx_ref[...], axis=1, keepdims=True)
        m0 = jnp.where(m == -jnp.inf, 0.0, m)
        p = jnp.exp2((s_ref[...] - m0) * (SCALE * LOG2E))
        l = jnp.sum(p, axis=1, keepdims=True)
        pv = lax.dot_general(p.astype(jnp.bfloat16), c[:lat, :], (((1,), (1,)), ((), ())), preferred_element_type=jnp.float32)
        has = l > 0.0
        l1 = jnp.where(has, l, 1.0)
        obuf[b] = (pv * (1.0 / l1)).astype(jnp.bfloat16)
        lse = jnp.where(has, m0 * SCALE + jnp.log(l1), -jnp.inf)
        lane = lax.broadcasted_iota(jnp.int32, lbuf.shape, 1)
        lbuf[...] = jnp.where(lane == b, lse, lbuf[...])

    lbuf[...] = jnp.zeros_like(lbuf)
    forward_q(0)
    forward_q(1)
    wait_q(0)
    cache_copy(0).wait()
    cache_copy(1).wait()
    scores(0, s_a, mx_a)
    scores(1, s_b, mx_b)
    values(0, s_a, mx_a)

    def body(k, _):
        @pl.when(k < pairs - 1)
        def _():
            forward_q(k + 1)

        wait_q(k)

        @pl.when(k < pairs - 2)
        def _():
            cache_copy(2 * k + 4).start()
            cache_copy(2 * k + 5).start()

        @pl.when(k > 1)
        def _():
            send_o(2 * k - 3)

        send_o(2 * k - 2)
        cache_copy(2 * k).wait()
        cache_copy(2 * k + 1).wait()
        scores(2 * k, s_a, mx_a)
        values(2 * k - 1, s_b, mx_b)
        scores(2 * k + 1, s_b, mx_b)
        values(2 * k, s_a, mx_a)
        return 0

    lax.fori_loop(1, pairs, body, 0)
    send_o(nb - 3)
    send_o(nb - 2)
    values(nb - 1, s_b, mx_b)
    for i in (1, 2, 0):
        l_copy(i, d, peers[i]).start()
    send_o(nb - 1)

    for i in (0, 1, 2):
        l_copy(i, peers[i], d).wait_recv()
    lses = [lbuf[rows(d), :]] + [lrecv[p] for p in peers]
    top = functools.reduce(jnp.maximum, lses)
    wts = [jnp.exp(x - top) for x in lses]
    norm = 1.0 / functools.reduce(jnp.add, wts)
    wts = [x * norm for x in wts]
    lane = lax.broadcasted_iota(jnp.int32, wts[0].shape, 1)

    def merge(k, _):
        for b in (2 * k, 2 * k + 1):
            for i in (0, 1, 2):
                o_copy(i, b, peers[i], d).wait_recv()
        for b in (2 * k, 2 * k + 1):
            parts = [obuf[b, rows(d), :]] + [orecv[p, b] for p in peers]
            total = None
            for w, o in zip(wts, parts):
                col = jnp.sum(jnp.where(lane == b, w, 0.0), axis=1, keepdims=True)
                term = col * o.astype(jnp.float32)
                total = term if total is None else total + term
            out_ref[b] = total.astype(jnp.bfloat16)
        return 0

    lax.fori_loop(0, pairs, merge, 0)

    for i in (0, 1, 2):
        l_copy(i, d, peers[i]).wait_send()

    def drain(b, _):
        for i in (0, 1, 2):
            o_copy(i, b, d, peers[i]).wait_send()
        return 0

    lax.fori_loop(0, nb, drain, 0)

    def drain_q(c, _):
        q_copy(0, c, d, mate).wait_send()
        q_copy(1, c, d, over).wait_send()
        q_copy(2, c, over, mate).wait_send()
        return 0

    lax.fori_loop(0, pairs, drain_q, 0)


def solution(mesh):
    n = mesh.shape['dcp']

    def local(q, cache, lengths):
        b, own, wd = q.shape
        sl = cache.shape[1]
        lat = wd - ROPE
        heads = own * n
        vmem = pl.BlockSpec(memory_space=pltpu.VMEM)
        return pl.pallas_call(
            kernel,
            out_shape=jax.ShapeDtypeStruct((b, own, lat), jnp.bfloat16),
            in_specs=[
                pl.BlockSpec(memory_space=pltpu.SMEM),
                pl.BlockSpec(memory_space=pl.ANY),
                pl.BlockSpec(memory_space=pl.ANY),
            ],
            out_specs=vmem,
            scratch_shapes=[
                pltpu.VMEM((SLOTS, wd, sl), jnp.bfloat16),
                pltpu.VMEM((b, heads, wd), jnp.bfloat16),
                pltpu.VMEM((heads, sl), jnp.float32),
                pltpu.VMEM((heads, sl), jnp.float32),
                pltpu.VMEM((heads, 128), jnp.float32),
                pltpu.VMEM((heads, 128), jnp.float32),
                pltpu.VMEM((b, heads, lat), jnp.bfloat16),
                pltpu.VMEM((n, b, own, lat), jnp.bfloat16),
                pltpu.VMEM((heads, 128), jnp.float32),
                pltpu.VMEM((n, own, 128), jnp.float32),
                pltpu.SemaphoreType.DMA((SLOTS,)),
                pltpu.SemaphoreType.DMA,
                pltpu.SemaphoreType.DMA((3, b // 2)),
                pltpu.SemaphoreType.DMA((3, b // 2)),
                pltpu.SemaphoreType.DMA((3, b)),
                pltpu.SemaphoreType.DMA((3, b)),
                pltpu.SemaphoreType.DMA((3,)),
                pltpu.SemaphoreType.DMA((3,)),
            ],
            compiler_params=pltpu.CompilerParams(
                collective_id=0, has_side_effects=True, vmem_limit_bytes=56 * 2 ** 20
            ),
            name='mla_decode',
        )(lengths, q, jnp.swapaxes(cache, 1, 2))

    return jax.shard_map(local, mesh=mesh, in_specs=(P('dp', 'dcp', None), P('dp', 'dcp', None), P('dp')), out_specs=P('dp', 'dcp', None), check_vma=False)
```

time: 152 us -> 59.6 us (0.39)
  matrix products: 65.7 us -> 0 us
  Pallas kernels: 0 us -> 57.1 us
  waiting for transfers between devices: 51.8 us -> 0 us
  between operations: 13.5 us -> 0.01 us
  other arithmetic: 10.8 us -> 0 us
  starting transfers between devices: 6.86 us -> 0 us
    dot_general x2 -> x0, matrix products: 65.7 us -> none  [the longest x1 33.4 us: partial_attention(): jnp.einsum('bhk,btk->bht', q, blk, preferred_element_type=jnp.float32)]
    pallas_call x0 -> x1, Pallas kernels: none -> 57.1 us  [local(): pl.pallas_call(kernel, out_shape=jax.ShapeDtypeStruct((b, own, lat), jnp....]
    all_gather x1 -> x0, waiting for transfers between devices: 27 us -> none  [local(): qa = lax.all_gather(q, 'dcp', axis=1, tiled=True)]
    all_to_all x2 -> x0, waiting for transfers between devices: 24 us -> none  [the longest x1 24 us: local(): od = lax.all_to_all(od, 'dcp', 1, 1, tiled=True)]
    reduce_sum x3 -> x0, other arithmetic: 9.29 us -> none  [the longest x1 8.02 us: partial_attention(): l = jnp.sum(p, axis=2)]
    all_to_all x2 -> x0, starting transfers between devices: 6.86 us -> none  [the longest x1 3.61 us: local(): od = lax.all_to_all(od, 'dcp', 1, 1, tiled=True)]
    reshape x1 -> x0, local copies, waits for them, and re-layouts: 1.58 us -> none  [local(): od = od.reshape(b, n, h // n, lat)]
  transfers between devices with their start and end apart: 3 -> 0, of which waited for: 2 -> 0; matrix products, arithmetic and copies ran while one was open for 24% -> 0% of each run, Pallas kernels for 0% -> 0%
where the time goes in v1:
time: 59.6 us; the launch traced here: 59 us
  Pallas kernels  57.1 us (96%)
  local copies, waits for them, and re-layouts  1.87 us (3%)
    pallas_call x1, Pallas kernels, local(): pl.pallas_call(kernel, out_shape=jax.ShapeDtypeStruct((b, own, lat), jnp....  57.1 us
    unnamed x1, local copies, waits for them, and re-layouts  1.87 us

profile of v1, /device:TPU:0, one launch (start us, length us, event | category | flops | bytes accessed | tf_op | source)
XLA Modules:
  0.0 59.0 jit_solution(16368707401233430917)
XLA Ops:
  0.0 57.1 %mla_decode.1 = bf16[32,16,512]{2,1,0:T(8,128)(2,1)} custom-call(s32[32]{0:T(128)} %len_ref.1, bf16[32,16,576]{2,1,0:T(8,128)(2,1)} %q_ref.1, bf16[32,576,2048]{2,1,0:T(8,128)(2,1)} %bitcast.cache_ref), custom_call_target="tpu_custom_call" | custom-call | tf_op jit(solution)/shard_map/mla_decode/pallas_call | solution.py:204
  57.1 1.9 %copy.5 = bf16[32,16,512]{2,1,0:T(8,128)(2,1)} copy(bf16[32,16,512]{2,1,0:T(8,128)(2,1)} %mla_decode.1) | data formatting | bytes 1048576

commit v2 on v1

v2 whole, which is shorter than its diff:
```python
import functools

import jax
import jax.numpy as jnp
from jax import lax
from jax.experimental import pallas as pl
from jax.experimental.pallas import tpu as pltpu
from jax.sharding import PartitionSpec as P

ROPE = 64
SCALE = 192 ** -0.5
LOG2E = 1.4426950408889634
SLOTS = 8
LEAD = 4
NT = (((1,), (1,)), ((), ()))


def kernel(len_ref, q_ref, cache_ref, out_ref, cbuf, qbuf, s_a, s_b, mx_a, mx_b, obuf, orecv, lbuf, lrecv,
           c_sem, q_sem, ms_sem, mr_sem, qs_sem, qr_sem, os_sem, or_sem, ls_sem, lr_sem):
    nb, heads, wd = qbuf.shape
    own = q_ref.shape[1]
    lat = wd - ROPE
    sl = cbuf.shape[2]
    pairs = nb // 2
    g = lax.axis_index('dp')
    d = lax.axis_index('dcp')
    mate = d + 1 - 2 * (d % 2)
    over = (d + 2) % 4
    far = mate + 2 - 4 * (mate // 2)
    peers = (mate, over, far)

    def rows(j):
        return pl.ds(pl.multiple_of(j * own, own), own)

    def cache_copy(b):
        slot = b % SLOTS
        return pltpu.make_async_copy(cache_ref.at[b], cbuf.at[slot], c_sem.at[slot])

    def remote(src, dst, ssem, rsem, dev):
        return pltpu.make_async_remote_copy(src_ref=src, dst_ref=dst, send_sem=ssem, recv_sem=rsem,
                                            device_id=(g, dev), device_id_type=pl.DeviceIdType.MESH)

    def mate_copy(i, src_dev, to):
        view = qbuf.at[pl.ds(0, 2) if i == 0 else pl.ds(2, nb - 2), rows(src_dev), :]
        return remote(view, view, ms_sem.at[i], mr_sem.at[i], to)

    def q_copy(kind, c, src_dev, to):
        view = qbuf.at[pl.ds(2 * c, 2), rows(src_dev), :]
        return remote(view, view, qs_sem.at[kind, c], qr_sem.at[kind, c], to)

    def o_copy(i, b, src_dev, dst_dev):
        return remote(obuf.at[b, rows(dst_dev), :], orecv.at[src_dev, b], os_sem.at[i, b], or_sem.at[i, b], dst_dev)

    def l_copy(t, i, src_dev, dst_dev):
        return remote(lbuf.at[t, rows(dst_dev), :], lrecv.at[t, src_dev], ls_sem.at[t, i], lr_sem.at[t, i], dst_dev)

    q_own = pltpu.make_async_copy(q_ref, qbuf.at[:, rows(d), :], q_sem)
    q_own.start()

    barrier = pltpu.get_barrier_semaphore()
    for p in peers:
        pl.semaphore_signal(barrier, inc=1, device_id=(g, p), device_id_type=pl.DeviceIdType.MESH)
    pl.semaphore_wait(barrier, 3)

    q_own.wait()
    q_copy(0, 0, d, over).start()
    mate_copy(0, d, mate).start()
    cache_copy(0).start()
    cache_copy(1).start()
    for c in range(1, LEAD):
        q_copy(0, c, d, over).start()
    mate_copy(1, d, mate).start()
    for b in range(2, 6):
        cache_copy(b).start()

    def forward_q(c):
        q_copy(0, c, over, over).wait_recv()
        q_copy(1, c, over, mate).start()

    def wait_q(c):
        q_copy(1, c, far, mate).wait_recv()

    def send_o(b):
        for i in (1, 2, 0):
            o_copy(i, b, d, peers[i]).start()

    def scores(b, s_ref, j, w, top):
        n_valid = len_ref[b] - d * sl
        c = cbuf.at[b % SLOTS]
        s = jnp.dot(qbuf[b], c[:, w * j:w * (j + 1)], preferred_element_type=jnp.float32)
        pos = lax.broadcasted_iota(jnp.int32, s.shape, 1) + w * j
        s = jnp.where(pos < n_valid, s, -jnp.inf)
        s_ref[:, w * j:w * (j + 1)] = s
        for k in range(w // 128):
            t = s[:, 128 * k:128 * (k + 1)]
            top = t if top is None else jnp.maximum(top, t)
        return top

    def weights(b, s_ref, mx_ref, src, dst):
        m = jnp.max(mx_ref[...], axis=1, keepdims=True)
        m0 = jnp.where(m == -jnp.inf, 0.0, m)
        p = jnp.exp2((s_ref[...] - m0) * (SCALE * LOG2E))
        l = jnp.sum(p, axis=1, keepdims=True)
        has = l > 0.0
        l1 = jnp.where(has, l, 1.0)
        lse = jnp.where(has, m0 * SCALE + jnp.log(l1), -jnp.inf)
        lane = lax.broadcasted_iota(jnp.int32, lbuf.shape[1:], 1)
        lbuf[dst] = jnp.where(lane == b, lse, lbuf[src])
        return p.astype(jnp.bfloat16), 1.0 / l1

    def values(b, pb, inv, m, w):
        c = cbuf.at[b % SLOTS]
        t = lax.dot_general(c[w * m:w * (m + 1), :], pb, NT, preferred_element_type=jnp.float32)
        obuf[b, :, w * m:w * (m + 1)] = (t.T * inv).astype(jnp.bfloat16)

    def step(bq, sq, mxq, bv, sv, mxv):
        if bv is not None:
            pb, inv = weights(bv, sv, mxv, 0, 0)
        top = None
        for j in range(8):
            top = scores(bq, sq, j, sl // 8, top)
            if bv is not None and j % 2 == 1:
                values(bv, pb, inv, j // 2, lat // 4)
        mxq[...] = top

    lbuf[0] = jnp.zeros(lbuf.shape[1:], jnp.float32)
    forward_q(0)
    mate_copy(0, mate, mate).wait_recv()
    cache_copy(0).wait()
    cache_copy(1).wait()
    forward_q(1)
    wait_q(0)
    step(0, s_a, mx_a, None, None, None)
    step(1, s_b, mx_b, 0, s_a, mx_a)
    mate_copy(1, mate, mate).wait_recv()

    def body(k, _):
        @pl.when(k < pairs - 1)
        def _():
            forward_q(k + 1)

        wait_q(k)

        @pl.when(k < pairs - LEAD + 1)
        def _():
            q_copy(0, k + LEAD - 1, d, over).start()

        @pl.when(k < pairs - 2)
        def _():
            cache_copy(2 * k + 4).start()
            cache_copy(2 * k + 5).start()

        @pl.when(k > 1)
        def _():
            send_o(2 * k - 3)

        send_o(2 * k - 2)
        cache_copy(2 * k).wait()
        cache_copy(2 * k + 1).wait()
        step(2 * k, s_a, mx_a, 2 * k - 1, s_b, mx_b)
        step(2 * k + 1, s_b, mx_b, 2 * k, s_a, mx_a)
        return 0

    lax.fori_loop(1, pairs, body, 0)

    def send_l(t):
        for i in (1, 2, 0):
            l_copy(t, i, d, peers[i]).start()

    send_o(nb - 3)
    send_o(nb - 2)
    send_l(0)
    pb, inv = weights(nb - 1, s_b, mx_b, 0, 1)
    for m in range(4):
        values(nb - 1, pb, inv, m, lat // 4)
    send_o(nb - 1)
    send_l(1)

    def shares(t):
        for i in (0, 1, 2):
            l_copy(t, i, peers[i], d).wait_recv()
        lses = [lbuf[t, rows(d), :]] + [lrecv[t, p] for p in peers]
        top = functools.reduce(jnp.maximum, lses)
        ws = [jnp.exp(x - top) for x in lses]
        norm = 1.0 / functools.reduce(jnp.add, ws)
        return [x * norm for x in ws]

    def merge(ws, b0):
        for b in (b0, b0 + 1):
            for i in (0, 1, 2):
                o_copy(i, b, peers[i], d).wait_recv()
        lane = lax.broadcasted_iota(jnp.int32, ws[0].shape, 1)
        for b in (b0, b0 + 1):
            parts = [obuf[b, rows(d), :]] + [orecv[p, b] for p in peers]
            total = None
            for w, o in zip(ws, parts):
                col = jnp.sum(jnp.where(lane == b, w, 0.0), axis=1, keepdims=True)
                term = col * o.astype(jnp.float32)
                total = term if total is None else total + term
            out_ref[b] = total.astype(jnp.bfloat16)

    early = shares(0)

    def merge_early(k, _):
        merge(early, 2 * k)
        return 0

    lax.fori_loop(0, pairs - 1, merge_early, 0)
    merge(shares(1), nb - 2)

    for t in (0, 1):
        for i in (0, 1, 2):
            l_copy(t, i, d, peers[i]).wait_send()
    for i in (0, 1):
        mate_copy(i, d, mate).wait_send()

    def drain(b, _):
        for i in (0, 1, 2):
            o_copy(i, b, d, peers[i]).wait_send()
        return 0

    lax.fori_loop(0, nb, drain, 0)

    def drain_q(c, _):
        q_copy(0, c, d, over).wait_send()
        q_copy(1, c, over, mate).wait_send()
        return 0

    lax.fori_loop(0, pairs, drain_q, 0)


def solution(mesh):
    n = mesh.shape['dcp']

    def local(q, cache, lengths):
        b, own, wd = q.shape
        sl = cache.shape[1]
        lat = wd - ROPE
        heads = own * n
        vmem = pl.BlockSpec(memory_space=pltpu.VMEM)
        return pl.pallas_call(
            kernel,
            out_shape=jax.ShapeDtypeStruct((b, own, lat), jnp.bfloat16),
            in_specs=[
                pl.BlockSpec(memory_space=pltpu.SMEM),
                pl.BlockSpec(memory_space=pltpu.HBM),
                pl.BlockSpec(memory_space=pltpu.HBM),
            ],
            out_specs=vmem,
            scratch_shapes=[
                pltpu.VMEM((SLOTS, wd, sl), jnp.bfloat16),
                pltpu.VMEM((b, heads, wd), jnp.bfloat16),
                pltpu.VMEM((heads, sl), jnp.float32),
                pltpu.VMEM((heads, sl), jnp.float32),
                pltpu.VMEM((heads, 128), jnp.float32),
                pltpu.VMEM((heads, 128), jnp.float32),
                pltpu.VMEM((b, heads, lat), jnp.bfloat16),
                pltpu.VMEM((n, b, own, lat), jnp.bfloat16),
                pltpu.VMEM((2, heads, 128), jnp.float32),
                pltpu.VMEM((2, n, own, 128), jnp.float32),
                pltpu.SemaphoreType.DMA((SLOTS,)),
                pltpu.SemaphoreType.DMA,
                pltpu.SemaphoreType.DMA((2,)),
                pltpu.SemaphoreType.DMA((2,)),
                pltpu.SemaphoreType.DMA((2, b // 2)),
                pltpu.SemaphoreType.DMA((2, b // 2)),
                pltpu.SemaphoreType.DMA((3, b)),
                pltpu.SemaphoreType.DMA((3, b)),
                pltpu.SemaphoreType.DMA((2, 3)),
                pltpu.SemaphoreType.DMA((2, 3)),
            ],
            compiler_params=pltpu.CompilerParams(
                collective_id=0, has_side_effects=True, vmem_limit_bytes=40 * 2 ** 20
            ),
            name='mla_decode',
        )(lengths, q, jnp.swapaxes(cache, 1, 2))

    return jax.shard_map(local, mesh=mesh, in_specs=(P('dp', 'dcp', None), P('dp', 'dcp', None), P('dp')), out_specs=P('dp', 'dcp', None), check_vma=False)
```

time: 59.6 us -> 53 us (0.89)
  Pallas kernels: 57.1 us -> 50.3 us
  local copies, waits for them, and re-layouts: 1.87 us -> 2.54 us
    pallas_call x1, Pallas kernels: 57.1 us -> 50.3 us  [local(): pl.pallas_call(kernel, out_shape=jax.ShapeDtypeStruct((b, own, lat), jnp....]
    unnamed x1 -> x5, local copies, waits for them, and re-layouts: 1.87 us -> 2.54 us
where the time goes in v2:
time: 53 us; the launch traced here: 52.9 us
  Pallas kernels  50.3 us (95%)
  local copies, waits for them, and re-layouts  2.54 us (5%)
    pallas_call x1, Pallas kernels, local(): pl.pallas_call(kernel, out_shape=jax.ShapeDtypeStruct((b, own, lat), jnp....  50.3 us
    unnamed x5, local copies, waits for them, and re-layouts  2.54 us

profile of v2, /device:TPU:0, one launch (start us, length us, event | category | flops | bytes accessed | tf_op | source)
XLA Modules:
  0.0 52.9 jit_solution(5571154668872164568)
XLA Ops:
  0.0 0.0 copy-start
  0.0 1.1 %copy-done = bf16[32,16,576]{2,1,0:T(8,128)(2,1)S(1)} copy-done((bf16[32,16,576]{2,1,0:T(8,128)(2,1)S(1)}, bf16[32,16,576]{2,1,0:T(8,128)(2,1)}, u32[]{:S(2)}) %copy-start) | copy-done | bytes 589848
  1.1 0.0 copy-start.1
  1.1 0.7 %copy-done.1 = s32[32]{0:T(128)S(1)} copy-done((s32[32]{0:T(128)S(1)}, s32[32]{0:T(128)}, u32[]{:S(2)}) %copy-start.1) | copy-done | bytes 152
  1.7 50.3 %mla_decode.1 = bf16[32,16,512]{2,1,0:T(8,128)(2,1)S(1)} custom-call(s32[32]{0:T(128)S(1)} %copy-done.1, bf16[32,16,576]{2,1,0:T(8,128)(2,1)S(1)} %copy-done, bf16[32,576,2048]{2,1,0:T(8,128)(2,1)} %bitcast.cache_ref), custom_call_target="tpu_custom_call" | custom-call | tf_op jit(solution)/shard_map/mla_decode/pallas_call | solution.py:241
  52.1 0.8 %copy.5 = bf16[32,16,512]{2,1,0:T(8,128)(2,1)} copy(bf16[32,16,512]{2,1,0:T(8,128)(2,1)S(1)} %mla_decode.1) | data formatting | bytes 1048576
Async XLA Ops:
  0.0 1.1 %copy-start = (bf16[32,16,576]{2,1,0:T(8,128)(2,1)S(1)}, bf16[32,16,576]{2,1,0:T(8,128)(2,1)}, u32[]{:S(2)}) copy-start(bf16[32,16,576]{2,1,0:T(8,128)(2,1)} %q_ref.1) | copy-start | bytes 1769476
  1.1 0.7 %copy-start.1 = (s32[32]{0:T(128)S(1)}, s32[32]{0:T(128)}, u32[]{:S(2)}) copy-start(s32[32]{0:T(128)} %len_ref.1) | copy-start | bytes 388

commit v3 on v2

--- a/solution.py
+++ b/solution.py
@@ -11,12 +11,12 @@
 SCALE = 192 ** -0.5
 LOG2E = 1.4426950408889634
 SLOTS = 8
-LEAD = 4
+LEAD = 5
 NT = (((1,), (1,)), ((), ()))
 
 
-def kernel(len_ref, q_ref, cache_ref, out_ref, cbuf, qbuf, s_a, s_b, mx_a, mx_b, obuf, orecv, lbuf, lrecv,
-           c_sem, q_sem, ms_sem, mr_sem, qs_sem, qr_sem, os_sem, or_sem, ls_sem, lr_sem):
+def kernel(lens_ref, q_ref, cache_ref, out_ref, cbuf, qbuf, s_a, s_b, mx_a, mx_b, obuf, orecv, lbuf, lrecv, len_ref,
+           n_sem, c_sem, q_sem, ms_sem, mr_sem, qs_sem, qr_sem, os_sem, or_sem, ls_sem, lr_sem):
     nb, heads, wd = qbuf.shape
     own = q_ref.shape[1]
     lat = wd - ROPE
@@ -48,14 +48,22 @@
         view = qbuf.at[pl.ds(2 * c, 2), rows(src_dev), :]
         return remote(view, view, qs_sem.at[kind, c], qr_sem.at[kind, c], to)
 
-    def o_copy(i, b, src_dev, dst_dev):
-        return remote(obuf.at[b, rows(dst_dev), :], orecv.at[src_dev, b], os_sem.at[i, b], or_sem.at[i, b], dst_dev)
+    def o_copy(i, c, src_dev, dst_dev):
+        if isinstance(c, int) and c in (0, pairs):
+            at = pl.ds(1, 1) if c == 0 else pl.ds(nb, 1)
+        else:
+            at = pl.ds(2 * c, 2)
+        return remote(obuf.at[at, rows(dst_dev), :], orecv.at[src_dev, at], os_sem.at[i, c], or_sem.at[i, c], dst_dev)
 
     def l_copy(t, i, src_dev, dst_dev):
         return remote(lbuf.at[t, rows(dst_dev), :], lrecv.at[t, src_dev], ls_sem.at[t, i], lr_sem.at[t, i], dst_dev)
 
     q_own = pltpu.make_async_copy(q_ref, qbuf.at[:, rows(d), :], q_sem)
     q_own.start()
+    lens = pltpu.make_async_copy(lens_ref, len_ref, n_sem)
+    lens.start()
+    cache_copy(0).start()
+    cache_copy(1).start()
 
     barrier = pltpu.get_barrier_semaphore()
     for p in peers:
@@ -65,8 +73,6 @@
     q_own.wait()
     q_copy(0, 0, d, over).start()
     mate_copy(0, d, mate).start()
-    cache_copy(0).start()
-    cache_copy(1).start()
     for c in range(1, LEAD):
         q_copy(0, c, d, over).start()
     mate_copy(1, d, mate).start()
@@ -80,9 +86,13 @@
     def wait_q(c):
         q_copy(1, c, far, mate).wait_recv()
 
-    def send_o(b):
+    def send_o(c):
         for i in (1, 2, 0):
-            o_copy(i, b, d, peers[i]).start()
+            o_copy(i, c, d, peers[i]).start()
+
+    def wait_o(c):
+        for i in (0, 1, 2):
+            o_copy(i, c, peers[i], d).wait_recv()
 
     def scores(b, s_ref, j, w, top):
         n_valid = len_ref[b] - d * sl
@@ -108,21 +118,29 @@
         lbuf[dst] = jnp.where(lane == b, lse, lbuf[src])
         return p.astype(jnp.bfloat16), 1.0 / l1
 
-    def values(b, pb, inv, m, w):
-        c = cbuf.at[b % SLOTS]
-        t = lax.dot_general(c[w * m:w * (m + 1), :], pb, NT, preferred_element_type=jnp.float32)
-        obuf[b, :, w * m:w * (m + 1)] = (t.T * inv).astype(jnp.bfloat16)
-
-    def step(bq, sq, mxq, bv, sv, mxv):
+    def step(bq, sq, mxq, bv, sv, mxv, dst=0):
+        tiles, chains = 8, 4
+        w, r = sl // tiles, lat // chains
         if bv is not None:
-            pb, inv = weights(bv, sv, mxv, 0, 0)
+            pb, inv = weights(bv, sv, mxv, 0, dst)
         top = None
-        for j in range(8):
-            top = scores(bq, sq, j, sl // 8, top)
-            if bv is not None and j % 2 == 1:
-                values(bv, pb, inv, j // 2, lat // 4)
-        mxq[...] = top
-
+        acc = [None] * chains
+        for j in range(tiles):
+            if bq is not None and j % 2 == 0:
+                top = scores(bq, sq, j // 2, 2 * w, top)
+            if bv is not None:
+                c = cbuf.at[bv % SLOTS]
+                for h in range(chains):
+                    t = lax.dot_general(c[r * h:r * (h + 1), w * j:w * (j + 1)], pb[:, w * j:w * (j + 1)], NT,
+                                        preferred_element_type=jnp.float32)
+                    acc[h] = t if j == 0 else acc[h] + t
+        if bv is not None:
+            for h in range(chains):
+                obuf[bv + 1, :, r * h:r * (h + 1)] = (acc[h].T * inv).astype(jnp.bfloat16)
+        if bq is not None:
+            mxq[...] = top
+
+    lens.wait()
     lbuf[0] = jnp.zeros(lbuf.shape[1:], jnp.float32)
     forward_q(0)
     mate_copy(0, mate, mate).wait_recv()
@@ -150,11 +168,14 @@
             cache_copy(2 * k + 4).start()
             cache_copy(2 * k + 5).start()
 
+        @pl.when(k == 1)
+        def _():
+            send_o(0)
+
         @pl.when(k > 1)
         def _():
-            send_o(2 * k - 3)
-
-        send_o(2 * k - 2)
+            send_o(k - 1)
+
         cache_copy(2 * k).wait()
         cache_copy(2 * k + 1).wait()
         step(2 * k, s_a, mx_a, 2 * k - 1, s_b, mx_b)
@@ -167,13 +188,10 @@
         for i in (1, 2, 0):
             l_copy(t, i, d, peers[i]).start()
 
-    send_o(nb - 3)
-    send_o(nb - 2)
+    send_o(pairs - 1)
     send_l(0)
-    pb, inv = weights(nb - 1, s_b, mx_b, 0, 1)
-    for m in range(4):
-        values(nb - 1, pb, inv, m, lat // 4)
-    send_o(nb - 1)
+    step(None, None, None, nb - 1, s_b, mx_b, 1)
+    send_o(pairs)
     send_l(1)
 
     def shares(t):
@@ -185,28 +203,32 @@
         norm = 1.0 / functools.reduce(jnp.add, ws)
         return [x * norm for x in ws]
 
-    def merge(ws, b0):
-        for b in (b0, b0 + 1):
-            for i in (0, 1, 2):
-                o_copy(i, b, peers[i], d).wait_recv()
+    def merge(ws, b):
         lane = lax.broadcasted_iota(jnp.int32, ws[0].shape, 1)
-        for b in (b0, b0 + 1):
-            parts = [obuf[b, rows(d), :]] + [orecv[p, b] for p in peers]
-            total = None
-            for w, o in zip(ws, parts):
-                col = jnp.sum(jnp.where(lane == b, w, 0.0), axis=1, keepdims=True)
-                term = col * o.astype(jnp.float32)
-                total = term if total is None else total + term
-            out_ref[b] = total.astype(jnp.bfloat16)
+        parts = [obuf[b + 1, rows(d), :]] + [orecv[p, b + 1] for p in peers]
+        total = None
+        for w, o in zip(ws, parts):
+            col = jnp.sum(jnp.where(lane == b, w, 0.0), axis=1, keepdims=True)
+            term = col * o.astype(jnp.float32)
+            total = term if total is None else total + term
+        out_ref[b] = total.astype(jnp.bfloat16)
 
     early = shares(0)
+    wait_o(0)
+    group = 6
 
     def merge_early(k, _):
-        merge(early, 2 * k)
+        for r in range(group // 2):
+            wait_o(group // 2 * k + r + 1)
+        for r in range(group):
+            merge(early, group * k + r)
         return 0
 
-    lax.fori_loop(0, pairs - 1, merge_early, 0)
-    merge(shares(1), nb - 2)
+    lax.fori_loop(0, (nb - 2) // group, merge_early, 0)
+    late = shares(1)
+    wait_o(pairs)
+    merge(late, nb - 2)
+    merge(late, nb - 1)
 
     for t in (0, 1):
         for i in (0, 1, 2):
@@ -214,12 +236,14 @@
     for i in (0, 1):
         mate_copy(i, d, mate).wait_send()
 
-    def drain(b, _):
+    def drain(c, _):
         for i in (0, 1, 2):
-            o_copy(i, b, d, peers[i]).wait_send()
+            o_copy(i, c, d, peers[i]).wait_send()
         return 0
 
-    lax.fori_loop(0, nb, drain, 0)
+    lax.fori_loop(1, pairs, drain, 0)
+    drain(0, 0)
+    drain(pairs, 0)
 
     def drain_q(c, _):
         q_copy(0, c, d, over).wait_send()
@@ -242,7 +266,7 @@
             kernel,
             out_shape=jax.ShapeDtypeStruct((b, own, lat), jnp.bfloat16),
             in_specs=[
-                pl.BlockSpec(memory_space=pltpu.SMEM),
+                pl.BlockSpec(memory_space=pltpu.HBM),
                 pl.BlockSpec(memory_space=pltpu.HBM),
                 pl.BlockSpec(memory_space=pltpu.HBM),
             ],
@@ -254,18 +278,20 @@
                 pltpu.VMEM((heads, sl), jnp.float32),
                 pltpu.VMEM((heads, 128), jnp.float32),
                 pltpu.VMEM((heads, 128), jnp.float32),
-                pltpu.VMEM((b, heads, lat), jnp.bfloat16),
-                pltpu.VMEM((n, b, own, lat), jnp.bfloat16),
+                pltpu.VMEM((b + 2, heads, lat), jnp.bfloat16),
+                pltpu.VMEM((n, b + 2, own, lat), jnp.bfloat16),
                 pltpu.VMEM((2, heads, 128), jnp.float32),
                 pltpu.VMEM((2, n, own, 128), jnp.float32),
+                pltpu.SMEM((b,), jnp.int32),
+                pltpu.SemaphoreType.DMA,
                 pltpu.SemaphoreType.DMA((SLOTS,)),
                 pltpu.SemaphoreType.DMA,
                 pltpu.SemaphoreType.DMA((2,)),
                 pltpu.SemaphoreType.DMA((2,)),
                 pltpu.SemaphoreType.DMA((2, b // 2)),
                 pltpu.SemaphoreType.DMA((2, b // 2)),
-                pltpu.SemaphoreType.DMA((3, b)),
-                pltpu.SemaphoreType.DMA((3, b)),
+                pltpu.SemaphoreType.DMA((3, b // 2 + 1)),
+                pltpu.SemaphoreType.DMA((3, b // 2 + 1)),
                 pltpu.SemaphoreType.DMA((2, 3)),
                 pltpu.SemaphoreType.DMA((2, 3)),
             ],
@@ -273,6 +299,6 @@
                 collective_id=0, has_side_effects=True, vmem_limit_bytes=40 * 2 ** 20
             ),
             name='mla_decode',
-        )(lengths, q, jnp.swapaxes(cache, 1, 2))
+        )(pltpu.with_memory_space_constraint(lengths, pltpu.HBM), pltpu.with_memory_space_constraint(q, pltpu.HBM), jnp.swapaxes(cache, 1, 2))
 
     return jax.shard_map(local, mesh=mesh, in_specs=(P('dp', 'dcp', None), P('dp', 'dcp', None), P('dp')), out_specs=P('dp', 'dcp', None), check_vma=False)

time: 53 us -> 48.8 us (0.921)
  Pallas kernels: 50.3 us -> 47.9 us
  local copies, waits for them, and re-layouts: 2.54 us -> 0.8 us
    pallas_call x1, Pallas kernels: 50.3 us -> 47.9 us  [local(): pl.pallas_call(kernel, out_shape=jax.ShapeDtypeStruct((b, own, lat), jnp....]
    unnamed x5 -> x1, local copies, waits for them, and re-layouts: 2.54 us -> 0.8 us
where the time goes in v3:
time: 48.8 us; the launch traced here: 48.7 us
  Pallas kernels  47.9 us (98%)
  local copies, waits for them, and re-layouts  0.8 us (2%)
    pallas_call x1, Pallas kernels, local(): pl.pallas_call(kernel, out_shape=jax.ShapeDtypeStruct((b, own, lat), jnp....  47.9 us

profile of v3, /device:TPU:0, one launch (start us, length us, event | category | flops | bytes accessed | tf_op | source)
XLA Modules:
  0.0 48.7 jit_solution(3562619274824850170)
XLA Ops:
  0.0 47.9 %mla_decode.1 = bf16[32,16,512]{2,1,0:T(8,128)(2,1)S(1)} custom-call(s32[32]{0:T(128)} %lens_ref.1, bf16[32,16,576]{2,1,0:T(8,128)(2,1)} %q_ref.1, bf16[32,576,2048]{2,1,0:T(8,128)(2,1)} %bitcast.cache_ref), custom_call_target="tpu_custom_call" | custom-call | tf_op jit(solution)/shard_map/mla_decode/pallas_call | solution.py:265
  47.9 0.8 %copy.5 = bf16[32,16,512]{2,1,0:T(8,128)(2,1)} copy(bf16[32,16,512]{2,1,0:T(8,128)(2,1)S(1)} %mla_decode.1) | data formatting | bytes 1048576

commit v4 on v3

v4 whole, which is shorter than its diff:
```python
import functools

import jax
import jax.numpy as jnp
from jax import lax
from jax.experimental import pallas as pl
from jax.experimental.pallas import tpu as pltpu
from jax.sharding import PartitionSpec as P

ROPE = 64
SCALE = 192 ** -0.5
LOG2E = 1.4426950408889634
SLOTS = 8
NT = (((1,), (1,)), ((), ()))


def kernel(lens_ref, q_ref, cache_ref, out_ref, cbuf, qbuf, rbuf, rown, s_a, s_b, mx_a, mx_b, obuf, orecv, lbuf, lrecv, len_ref,
           n_sem, c_sem, q_sem, ms_sem, mr_sem, qs_sem, qr_sem, rs_sem, rr_sem, os_sem, or_sem, ls_sem, lr_sem):
    nb, heads, lat = qbuf.shape
    own = q_ref.shape[1]
    sl = cbuf.shape[2]
    pairs = nb // 2
    g = lax.axis_index('dp')
    d = lax.axis_index('dcp')
    mate = d + 1 - 2 * (d % 2)
    over = (d + 2) % 4
    far = mate + 2 - 4 * (mate // 2)
    peers = (mate, over, far)

    def rows(j):
        return pl.ds(pl.multiple_of(j * own, own), own)

    def cache_copy(b):
        slot = b % SLOTS
        return pltpu.make_async_copy(cache_ref.at[b], cbuf.at[slot], c_sem.at[slot])

    def remote(src, dst, ssem, rsem, dev):
        return pltpu.make_async_remote_copy(src_ref=src, dst_ref=dst, send_sem=ssem, recv_sem=rsem,
                                            device_id=(g, dev), device_id_type=pl.DeviceIdType.MESH)

    def seqs(m):
        if isinstance(m, int) and m < 2:
            return pl.ds(2 * m, 2)
        return pl.ds(4 * m - 4, 4)

    def q_copy(kind, m, src_dev, to):
        view = qbuf.at[seqs(m), rows(src_dev), :]
        return remote(view, view, qs_sem.at[kind, m], qr_sem.at[kind, m], to)

    def r_copy(kind, i, src_dev, to):
        view = rbuf.at[pl.ds(0, 2) if i == 0 else pl.ds(2, pairs - 2), rows(src_dev), :]
        return remote(view, view, rs_sem.at[kind, i], rr_sem.at[kind, i], to)

    def mate_copy(i, src_dev, to):
        if i == 2:
            view = rbuf.at[:, rows(src_dev), :]
        else:
            view = qbuf.at[pl.ds(0, 2) if i == 0 else pl.ds(2, nb - 2), rows(src_dev), :]
        return remote(view, view, ms_sem.at[i], mr_sem.at[i], to)

    last = nb // 4

    def o_copy(i, c, src_dev, dst_dev):
        if isinstance(c, int) and c in (0, last, last + 1):
            at = {0: pl.ds(1, 1), last: pl.ds(nb - 2, 2), last + 1: pl.ds(nb, 1)}[c]
        else:
            at = pl.ds(4 * c - 2, 4)
        return remote(obuf.at[at, rows(dst_dev), :], orecv.at[src_dev, at], os_sem.at[i, c], or_sem.at[i, c], dst_dev)

    def l_copy(t, i, src_dev, dst_dev):
        return remote(lbuf.at[t, rows(dst_dev), :], lrecv.at[t, src_dev], ls_sem.at[t, i], lr_sem.at[t, i], dst_dev)

    r_own = pltpu.make_async_copy(q_ref.at[:, :, pl.ds(lat, ROPE)], rown, q_sem.at[0])
    r_own.start()
    q_own = pltpu.make_async_copy(q_ref.at[:, :, pl.ds(0, lat)], qbuf.at[:, rows(d), :], q_sem.at[1])
    q_own.start()
    lens = pltpu.make_async_copy(lens_ref, len_ref, n_sem)
    lens.start()
    cache_copy(0).start()
    cache_copy(1).start()

    barrier = pltpu.get_barrier_semaphore()
    for p in peers:
        pl.semaphore_signal(barrier, inc=1, device_id=(g, p), device_id_type=pl.DeviceIdType.MESH)
    r_own.wait()
    for c in range(pairs):
        rbuf[c, rows(d), :] = jnp.concatenate([rown[2 * c], rown[2 * c + 1]], axis=1)
    lbuf[0] = jnp.zeros(lbuf.shape[1:], jnp.float32)
    pl.semaphore_wait(barrier, 3)

    q_own.wait()
    q_copy(0, 0, d, over).start()
    r_copy(0, 0, d, over).start()
    mate_copy(2, d, mate).start()
    mate_copy(0, d, mate).start()
    q_copy(0, 1, d, over).start()
    q_copy(0, 2, d, over).start()
    r_copy(0, 1, d, over).start()
    q_copy(0, 3, d, over).start()
    mate_copy(1, d, mate).start()
    for b in range(2, 6):
        cache_copy(b).start()

    def forward_q(m):
        q_copy(0, m, over, over).wait_recv()
        q_copy(1, m, over, mate).start()

    def forward_r(i):
        r_copy(0, i, over, over).wait_recv()
        r_copy(1, i, over, mate).start()

    def send_o(c):
        for i in (1, 2, 0):
            o_copy(i, c, d, peers[i]).start()

    def wait_o(c):
        for i in (0, 1, 2):
            o_copy(i, c, peers[i], d).wait_recv()

    def scores(k, odd, s_ref, j, w, top):
        b = 2 * k + odd
        n_valid = len_ref[b] - d * sl
        c = cbuf.at[b % SLOTS]
        q = jnp.concatenate([qbuf[b], rbuf[k, :, ROPE * odd:ROPE * (odd + 1)]], axis=1)
        s = jnp.dot(q, c[:, w * j:w * (j + 1)], preferred_element_type=jnp.float32)
        pos = lax.broadcasted_iota(jnp.int32, s.shape, 1) + w * j
        s = jnp.where(pos < n_valid, s, -jnp.inf)
        s_ref[:, w * j:w * (j + 1)] = s
        for k in range(w // 128):
            t = s[:, 128 * k:128 * (k + 1)]
            top = t if top is None else jnp.maximum(top, t)
        return top

    def weights(b, s_ref, mx_ref, src, dst):
        m = jnp.max(mx_ref[...], axis=1, keepdims=True)
        m0 = jnp.where(m == -jnp.inf, 0.0, m)
        p = jnp.exp2((s_ref[...] - m0) * (SCALE * LOG2E))
        l = jnp.sum(p, axis=1, keepdims=True)
        has = l > 0.0
        l1 = jnp.where(has, l, 1.0)
        lse = jnp.where(has, m0 * SCALE + jnp.log(l1), -jnp.inf)
        lane = lax.broadcasted_iota(jnp.int32, lbuf.shape[1:], 1)
        lbuf[dst] = jnp.where(lane == b, lse, lbuf[src])
        return p.astype(jnp.bfloat16), 1.0 / l1

    def step(kq, odd, sq, mxq, bv, sv, mxv, dst=0):
        tiles, chains = 8, 4
        w, r = sl // tiles, lat // chains
        if bv is not None:
            pb, inv = weights(bv, sv, mxv, 0, dst)
        top = None
        acc = [None] * chains
        for j in range(tiles):
            if kq is not None and j % 2 == 0:
                top = scores(kq, odd, sq, j // 2, 2 * w, top)
            if bv is not None:
                c = cbuf.at[bv % SLOTS]
                for h in range(chains):
                    t = lax.dot_general(c[r * h:r * (h + 1), w * j:w * (j + 1)], pb[:, w * j:w * (j + 1)], NT,
                                        preferred_element_type=jnp.float32)
                    acc[h] = t if j == 0 else acc[h] + t
        if bv is not None:
            for h in range(chains):
                obuf[bv + 1, :, r * h:r * (h + 1)] = (acc[h].T * inv).astype(jnp.bfloat16)
        if kq is not None:
            mxq[...] = top

    lens.wait()
    forward_q(0)
    forward_r(0)
    mate_copy(0, mate, mate).wait_recv()
    mate_copy(2, mate, mate).wait_recv()
    cache_copy(0).wait()
    cache_copy(1).wait()
    forward_q(1)
    q_copy(1, 0, far, mate).wait_recv()
    r_copy(1, 0, far, mate).wait_recv()
    step(0, 0, s_a, mx_a, None, None, None)
    step(0, 1, s_b, mx_b, 0, s_a, mx_a)
    mate_copy(1, mate, mate).wait_recv()

    def body(k, _):
        odd = k % 2 == 1

        @pl.when(k == 1)
        def _():
            forward_r(1)
            send_o(0)
            q_copy(1, 1, far, mate).wait_recv()

        @pl.when(jnp.logical_and(odd, k < pairs - 1))
        def _():
            forward_q((k + 1) // 2 + 1)

        @pl.when(jnp.logical_and(odd, k > 1))
        def _():
            send_o((k - 1) // 2)

        @pl.when(jnp.logical_and(odd, k < pairs - 6))
        def _():
            q_copy(0, (k - 1) // 2 + 4, d, over).start()

        @pl.when(k == 2)
        def _():
            r_copy(1, 1, far, mate).wait_recv()

        @pl.when(k % 2 == 0)
        def _():
            q_copy(1, k // 2 + 1, far, mate).wait_recv()

        @pl.when(k < pairs - 2)
        def _():
            cache_copy(2 * k + 4).start()
            cache_copy(2 * k + 5).start()

        cache_copy(2 * k).wait()
        cache_copy(2 * k + 1).wait()
        step(k, 0, s_a, mx_a, 2 * k - 1, s_b, mx_b)
        step(k, 1, s_b, mx_b, 2 * k, s_a, mx_a)
        return 0

    lax.fori_loop(1, pairs, body, 0)

    def send_l(t):
        for i in (1, 2, 0):
            l_copy(t, i, d, peers[i]).start()

    send_o(last)
    send_l(0)
    step(None, None, None, None, nb - 1, s_b, mx_b, 1)
    send_o(last + 1)
    send_l(1)

    def shares(t):
        for i in (0, 1, 2):
            l_copy(t, i, peers[i], d).wait_recv()
        lses = [lbuf[t, rows(d), :]] + [lrecv[t, p] for p in peers]
        top = functools.reduce(jnp.maximum, lses)
        ws = [jnp.exp(x - top) for x in lses]
        norm = 1.0 / functools.reduce(jnp.add, ws)
        return [x * norm for x in ws]

    def merge(ws, b):
        lane = lax.broadcasted_iota(jnp.int32, ws[0].shape, 1)
        parts = [obuf[b + 1, rows(d), :]] + [orecv[p, b + 1] for p in peers]
        total = None
        for w, o in zip(ws, parts):
            col = jnp.sum(jnp.where(lane == b, w, 0.0), axis=1, keepdims=True)
            term = col * o.astype(jnp.float32)
            total = term if total is None else total + term
        out_ref[b] = total.astype(jnp.bfloat16)

    early = shares(0)
    wait_o(0)
    merge(early, 0)

    def merge_early(m, _):
        wait_o(m)
        for r in range(4):
            merge(early, 4 * m - 3 + r)
        return 0

    lax.fori_loop(1, last, merge_early, 0)
    wait_o(last)
    merge(early, nb - 3)
    merge(early, nb - 2)
    late = shares(1)
    wait_o(last + 1)
    merge(late, nb - 1)

    for t in (0, 1):
        for i in (0, 1, 2):
            l_copy(t, i, d, peers[i]).wait_send()
    for i in (0, 1, 2):
        mate_copy(i, d, mate).wait_send()

    def drain(c, _):
        for i in (0, 1, 2):
            o_copy(i, c, d, peers[i]).wait_send()
        return 0

    lax.fori_loop(1, last, drain, 0)
    for c in (0, last, last + 1):
        drain(c, 0)

    def drain_q(m, _):
        q_copy(0, m, d, over).wait_send()
        q_copy(1, m, over, mate).wait_send()
        return 0

    lax.fori_loop(2, pairs // 2 + 1, drain_q, 0)
    for m in (0, 1):
        drain_q(m, 0)
        r_copy(0, m, d, over).wait_send()
        r_copy(1, m, over, mate).wait_send()


def solution(mesh):
    n = mesh.shape['dcp']

    def local(q, cache, lengths):
        b, own, wd = q.shape
        sl = cache.shape[1]
        lat = wd - ROPE
        heads = own * n
        vmem = pl.BlockSpec(memory_space=pltpu.VMEM)
        dma = pltpu.SemaphoreType.DMA
        return pl.pallas_call(
            kernel,
            out_shape=jax.ShapeDtypeStruct((b, own, lat), jnp.bfloat16),
            in_specs=[
                pl.BlockSpec(memory_space=pltpu.HBM),
                pl.BlockSpec(memory_space=pltpu.HBM),
                pl.BlockSpec(memory_space=pltpu.HBM),
            ],
            out_specs=vmem,
            scratch_shapes=[
                pltpu.VMEM((SLOTS, wd, sl), jnp.bfloat16),
                pltpu.VMEM((b, heads, lat), jnp.bfloat16),
                pltpu.VMEM((b // 2, heads, 2 * ROPE), jnp.bfloat16),
                pltpu.VMEM((b, own, ROPE), jnp.bfloat16),
                pltpu.VMEM((heads, sl), jnp.float32),
                pltpu.VMEM((heads, sl), jnp.float32),
                pltpu.VMEM((heads, 128), jnp.float32),
                pltpu.VMEM((heads, 128), jnp.float32),
                pltpu.VMEM((b + 2, heads, lat), jnp.bfloat16),
                pltpu.VMEM((n, b + 2, own, lat), jnp.bfloat16),
                pltpu.VMEM((2, heads, 128), jnp.float32),
                pltpu.VMEM((2, n, own, 128), jnp.float32),
                pltpu.SMEM((b,), jnp.int32),
                dma,
                dma((SLOTS,)),
                dma((2,)),
                dma((3,)),
                dma((3,)),
                dma((2, b // 4 + 1)),
                dma((2, b // 4 + 1)),
                dma((2, 2)),
                dma((2, 2)),
                dma((3, b // 4 + 2)),
                dma((3, b // 4 + 2)),
                dma((2, 3)),
                dma((2, 3)),
            ],
            compiler_params=pltpu.CompilerParams(
                collective_id=0, has_side_effects=True, vmem_limit_bytes=40 * 2 ** 20
            ),
            name='mla_decode',
        )(pltpu.with_memory_space_constraint(lengths, pltpu.HBM), pltpu.with_memory_space_constraint(q, pltpu.HBM), jnp.swapaxes(cache, 1, 2))

    return jax.shard_map(local, mesh=mesh, in_specs=(P('dp', 'dcp', None), P('dp', 'dcp', None), P('dp')), out_specs=P('dp', 'dcp', None), check_vma=False)
```

time: 48.8 us -> 50.1 us (1.027)
  Pallas kernels: 47.9 us -> 49.2 us
    pallas_call x1, Pallas kernels: 47.9 us -> 49.2 us  [local(): pl.pallas_call(kernel, out_shape=jax.ShapeDtypeStruct((b, own, lat), jnp....]
where the time goes in v4:
time: 50.1 us; the launch traced here: 50 us
  Pallas kernels  49.2 us (98%)
  local copies, waits for them, and re-layouts  0.8 us (2%)
    pallas_call x1, Pallas kernels, local(): pl.pallas_call(kernel, out_shape=jax.ShapeDtypeStruct((b, own, lat), jnp....  49.2 us

profile of v4, /device:TPU:0, one launch (start us, length us, event | category | flops | bytes accessed | tf_op | source)
XLA Modules:
  0.0 50.0 jit_solution(1853036804507181243)
XLA Ops:
  0.0 49.2 %mla_decode.1 = bf16[32,16,512]{2,1,0:T(8,128)(2,1)S(1)} custom-call(s32[32]{0:T(128)} %lens_ref.1, bf16[32,16,576]{2,1,0:T(8,128)(2,1)} %q_ref.1, bf16[32,576,2048]{2,1,0:T(8,128)(2,1)} %bitcast.cache_ref), custom_call_target="tpu_custom_call" | custom-call | tf_op jit(solution)/shard_map/mla_decode/pallas_call | solution.py:308
  49.2 0.8 %copy.5 = bf16[32,16,512]{2,1,0:T(8,128)(2,1)} copy(bf16[32,16,512]{2,1,0:T(8,128)(2,1)S(1)} %mla_decode.1) | data formatting | bytes 1048576

commit v5 on v3

--- a/solution.py
+++ b/solution.py
@@ -49,8 +49,8 @@
         return remote(view, view, qs_sem.at[kind, c], qr_sem.at[kind, c], to)
 
     def o_copy(i, c, src_dev, dst_dev):
-        if isinstance(c, int) and c in (0, pairs):
-            at = pl.ds(1, 1) if c == 0 else pl.ds(nb, 1)
+        if isinstance(c, int) and (c == 0 or c >= pairs - 1):
+            at = pl.ds(1 if c == 0 else c + pairs - 1, 1)
         else:
             at = pl.ds(2 * c, 2)
         return remote(obuf.at[at, rows(dst_dev), :], orecv.at[src_dev, at], os_sem.at[i, c], or_sem.at[i, c], dst_dev)
@@ -62,8 +62,6 @@
     q_own.start()
     lens = pltpu.make_async_copy(lens_ref, len_ref, n_sem)
     lens.start()
-    cache_copy(0).start()
-    cache_copy(1).start()
 
     barrier = pltpu.get_barrier_semaphore()
     for p in peers:
@@ -73,11 +71,10 @@
     q_own.wait()
     q_copy(0, 0, d, over).start()
     mate_copy(0, d, mate).start()
+    cache_copy(0).start()
     for c in range(1, LEAD):
         q_copy(0, c, d, over).start()
-    mate_copy(1, d, mate).start()
-    for b in range(2, 6):
-        cache_copy(b).start()
+    cache_copy(1).start()
 
     def forward_q(c):
         q_copy(0, c, over, over).wait_recv()
@@ -118,17 +115,17 @@
         lbuf[dst] = jnp.where(lane == b, lse, lbuf[src])
         return p.astype(jnp.bfloat16), 1.0 / l1
 
-    def step(bq, sq, mxq, bv, sv, mxv, dst=0):
+    def step(bq, sq, mxq, bv, sv, mxv, dst=0, at=(0, 2, 4, 6)):
         tiles, chains = 8, 4
         w, r = sl // tiles, lat // chains
         if bv is not None:
             pb, inv = weights(bv, sv, mxv, 0, dst)
         top = None
         acc = [None] * chains
-        for j in range(tiles):
-            if bq is not None and j % 2 == 0:
-                top = scores(bq, sq, j // 2, 2 * w, top)
-            if bv is not None:
+        for j in range(tiles + 1):
+            if bq is not None and j in at:
+                top = scores(bq, sq, at.index(j), 2 * w, top)
+            if bv is not None and j < tiles:
                 c = cbuf.at[bv % SLOTS]
                 for h in range(chains):
                     t = lax.dot_general(c[r * h:r * (h + 1), w * j:w * (j + 1)], pb[:, w * j:w * (j + 1)], NT,
@@ -140,58 +137,79 @@
         if bq is not None:
             mxq[...] = top
 
+    lbuf[0] = jnp.zeros(lbuf.shape[1:], jnp.float32)
     lens.wait()
-    lbuf[0] = jnp.zeros(lbuf.shape[1:], jnp.float32)
     forward_q(0)
+    mate_copy(1, d, mate).start()
+    cache_copy(2).start()
+    cache_copy(3).start()
     mate_copy(0, mate, mate).wait_recv()
     cache_copy(0).wait()
     cache_copy(1).wait()
     forward_q(1)
+    cache_copy(4).start()
+    cache_copy(5).start()
     wait_q(0)
     step(0, s_a, mx_a, None, None, None)
     step(1, s_b, mx_b, 0, s_a, mx_a)
     mate_copy(1, mate, mate).wait_recv()
 
-    def body(k, _):
-        @pl.when(k < pairs - 1)
-        def _():
-            forward_q(k + 1)
+    def enter(k):
+        if not isinstance(k, int):
+            @pl.when(k < pairs - 1)
+            def _():
+                forward_q(k + 1)
 
         wait_q(k)
-
-        @pl.when(k < pairs - LEAD + 1)
-        def _():
-            q_copy(0, k + LEAD - 1, d, over).start()
-
-        @pl.when(k < pairs - 2)
-        def _():
-            cache_copy(2 * k + 4).start()
-            cache_copy(2 * k + 5).start()
-
-        @pl.when(k == 1)
-        def _():
-            send_o(0)
-
-        @pl.when(k > 1)
-        def _():
+        if not isinstance(k, int):
+            @pl.when(k < pairs - LEAD + 1)
+            def _():
+                q_copy(0, k + LEAD - 1, d, over).start()
+
+            @pl.when(k < pairs - 2)
+            def _():
+                cache_copy(2 * k + 4).start()
+                cache_copy(2 * k + 5).start()
+
+            @pl.when(k == 1)
+            def _():
+                send_o(0)
+
+            @pl.when(k > 1)
+            def _():
+                send_o(k - 1)
+        else:
             send_o(k - 1)
 
         cache_copy(2 * k).wait()
         cache_copy(2 * k + 1).wait()
+
+    def first(k):
         step(2 * k, s_a, mx_a, 2 * k - 1, s_b, mx_b)
-        step(2 * k + 1, s_b, mx_b, 2 * k, s_a, mx_a)
+
+    def second(k):
+        step(2 * k + 1, s_b, mx_b, 2 * k, s_a, mx_a, at=(0, 2, 4, 8))
+
+    def body(k, _):
+        enter(k)
+        first(k)
+        second(k)
         return 0
 
-    lax.fori_loop(1, pairs, body, 0)
+    lax.fori_loop(1, pairs - 1, body, 0)
 
     def send_l(t):
         for i in (1, 2, 0):
             l_copy(t, i, d, peers[i]).start()
 
+    enter(pairs - 1)
+    first(pairs - 1)
     send_o(pairs - 1)
+    second(pairs - 1)
+    send_o(pairs)
     send_l(0)
     step(None, None, None, nb - 1, s_b, mx_b, 1)
-    send_o(pairs)
+    send_o(pairs + 1)
     send_l(1)
 
     def shares(t):
@@ -224,10 +242,17 @@
             merge(early, group * k + r)
         return 0
 
-    lax.fori_loop(0, (nb - 2) // group, merge_early, 0)
+    whole = (nb - 3) // group
+    lax.fori_loop(0, whole, merge_early, 0)
+    for c in range(group // 2 * whole + 1, pairs - 1):
+        wait_o(c)
+    for b in range(group * whole, nb - 3):
+        merge(early, b)
+    for b in (nb - 3, nb - 2):
+        wait_o(b - pairs + 2)
+        merge(early, b)
     late = shares(1)
-    wait_o(pairs)
-    merge(late, nb - 2)
+    wait_o(pairs + 1)
     merge(late, nb - 1)
 
     for t in (0, 1):
@@ -241,9 +266,9 @@
             o_copy(i, c, d, peers[i]).wait_send()
         return 0
 
-    lax.fori_loop(1, pairs, drain, 0)
-    drain(0, 0)
-    drain(pairs, 0)
+    lax.fori_loop(1, pairs - 1, drain, 0)
+    for c in (0, pairs - 1, pairs, pairs + 1):
+        drain(c, 0)
 
     def drain_q(c, _):
         q_copy(0, c, d, over).wait_send()
@@ -290,8 +315,8 @@
                 pltpu.SemaphoreType.DMA((2,)),
                 pltpu.SemaphoreType.DMA((2, b // 2)),
                 pltpu.SemaphoreType.DMA((2, b // 2)),
-                pltpu.SemaphoreType.DMA((3, b // 2 + 1)),
-                pltpu.SemaphoreType.DMA((3, b // 2 + 1)),
+                pltpu.SemaphoreType.DMA((3, b // 2 + 2)),
+                pltpu.SemaphoreType.DMA((3, b // 2 + 2)),
                 pltpu.SemaphoreType.DMA((2, 3)),
                 pltpu.SemaphoreType.DMA((2, 3)),
             ],

time: 48.8 us -> 47.7 us (0.977)
  Pallas kernels: 47.9 us -> 46.8 us
    pallas_call x1, Pallas kernels: 47.9 us -> 46.8 us  [local(): pl.pallas_call(kernel, out_shape=jax.ShapeDtypeStruct((b, own, lat), jnp....]
where the time goes in v5:
time: 47.7 us; the launch traced here: 47.6 us
  Pallas kernels  46.8 us (98%)
  local copies, waits for them, and re-layouts  0.8 us (2%)
    pallas_call x1, Pallas kernels, local(): pl.pallas_call(kernel, out_shape=jax.ShapeDtypeStruct((b, own, lat), jnp....  46.8 us

profile of v5, /device:TPU:0, one launch (start us, length us, event | category | flops | bytes accessed | tf_op | source)
XLA Modules:
  0.0 47.6 jit_solution(8203026000939419936)
XLA Ops:
  0.0 46.8 %mla_decode.1 = bf16[32,16,512]{2,1,0:T(8,128)(2,1)S(1)} custom-call(s32[32]{0:T(128)} %lens_ref.1, bf16[32,16,576]{2,1,0:T(8,128)(2,1)} %q_ref.1, bf16[32,576,2048]{2,1,0:T(8,128)(2,1)} %bitcast.cache_ref), custom_call_target="tpu_custom_call" | custom-call | tf_op jit(solution)/shard_map/mla_decode/pallas_call | solution.py:290
  46.8 0.8 %copy.5 = bf16[32,16,512]{2,1,0:T(8,128)(2,1)} copy(bf16[32,16,512]{2,1,0:T(8,128)(2,1)S(1)} %mla_decode.1) | data formatting | bytes 1048576

commit v6 on v5

--- a/solution.py
+++ b/solution.py
@@ -10,8 +10,8 @@
 ROPE = 64
 SCALE = 192 ** -0.5
 LOG2E = 1.4426950408889634
-SLOTS = 8
-LEAD = 5
+SLOTS = 12
+LEAD = 7
 NT = (((1,), (1,)), ((), ()))
 
 
@@ -48,11 +48,13 @@
         view = qbuf.at[pl.ds(2 * c, 2), rows(src_dev), :]
         return remote(view, view, qs_sem.at[kind, c], qr_sem.at[kind, c], to)
 
+    quads = nb // 4
+
     def o_copy(i, c, src_dev, dst_dev):
-        if isinstance(c, int) and (c == 0 or c >= pairs - 1):
-            at = pl.ds(1 if c == 0 else c + pairs - 1, 1)
+        if isinstance(c, int) and (c == 0 or c >= quads):
+            at = pl.ds(1 if c == 0 else c + nb - 2 - quads, 1)
         else:
-            at = pl.ds(2 * c, 2)
+            at = pl.ds(4 * c - 2, 4)
         return remote(obuf.at[at, rows(dst_dev), :], orecv.at[src_dev, at], os_sem.at[i, c], or_sem.at[i, c], dst_dev)
 
     def l_copy(t, i, src_dev, dst_dev):
@@ -146,70 +148,75 @@
     mate_copy(0, mate, mate).wait_recv()
     cache_copy(0).wait()
     cache_copy(1).wait()
+    wait_q(0)
+    step(0, s_a, mx_a, None, None, None)
     forward_q(1)
+    forward_q(2)
     cache_copy(4).start()
     cache_copy(5).start()
-    wait_q(0)
-    step(0, s_a, mx_a, None, None, None)
     step(1, s_b, mx_b, 0, s_a, mx_a)
     mate_copy(1, mate, mate).wait_recv()
 
-    def enter(k):
-        if not isinstance(k, int):
-            @pl.when(k < pairs - 1)
+    def enter(m):
+        for c in (2 * m + 3, 2 * m + 4):
+            @pl.when(c < pairs)
             def _():
-                forward_q(k + 1)
-
-        wait_q(k)
-        if not isinstance(k, int):
-            @pl.when(k < pairs - LEAD + 1)
+                forward_q(c)
+
+        for c in (2 * m + LEAD, 2 * m + LEAD + 1):
+            @pl.when(c < pairs)
             def _():
-                q_copy(0, k + LEAD - 1, d, over).start()
-
-            @pl.when(k < pairs - 2)
+                q_copy(0, c, d, over).start()
+
+        @pl.when(m == 0)
+        def _():
+            send_o(0)
+
+        @pl.when(m > 0)
+        def _():
+            send_o(m)
+
+        for b in range(6, 10):
+            @pl.when(4 * m + b < nb)
             def _():
-                cache_copy(2 * k + 4).start()
-                cache_copy(2 * k + 5).start()
-
-            @pl.when(k == 1)
-            def _():
-                send_o(0)
-
-            @pl.when(k > 1)
-            def _():
-                send_o(k - 1)
-        else:
-            send_o(k - 1)
-
-        cache_copy(2 * k).wait()
-        cache_copy(2 * k + 1).wait()
-
-    def first(k):
-        step(2 * k, s_a, mx_a, 2 * k - 1, s_b, mx_b)
-
-    def second(k):
-        step(2 * k + 1, s_b, mx_b, 2 * k, s_a, mx_a, at=(0, 2, 4, 8))
-
-    def body(k, _):
-        enter(k)
-        first(k)
-        second(k)
+                cache_copy(4 * m + b).start()
+
+        for c in (1, 2):
+            wait_q(2 * m + c)
+        for b in range(2, 6):
+            cache_copy(4 * m + b).wait()
+
+    def first(k, at=(0,2,4,6)):
+        step(2 * k, s_a, mx_a, 2 * k - 1, s_b, mx_b, at=at)
+
+    def second(k, at=(0,2,4,8)):
+        step(2 * k + 1, s_b, mx_b, 2 * k, s_a, mx_a, at=at)
+
+    def body(m, _):
+        enter(m)
+        first(2 * m + 1)
+        second(2 * m + 1, (0,2,4,6))
+        first(2 * m + 2)
+        second(2 * m + 2)
         return 0
 
-    lax.fori_loop(1, pairs - 1, body, 0)
+    lax.fori_loop(0, quads - 1, body, 0)
 
     def send_l(t):
         for i in (1, 2, 0):
             l_copy(t, i, d, peers[i]).start()
 
-    enter(pairs - 1)
+    send_o(quads - 1)
+    wait_q(pairs - 1)
+    cache_copy(nb - 2).wait()
+    cache_copy(nb - 1).wait()
     first(pairs - 1)
-    send_o(pairs - 1)
+    send_o(quads)
     second(pairs - 1)
-    send_o(pairs)
+    send_o(quads + 1)
     send_l(0)
     step(None, None, None, nb - 1, s_b, mx_b, 1)
-    send_o(pairs + 1)
+    send_o(quads + 2)
     send_l(1)
 
     def shares(t):
@@ -233,26 +240,24 @@
 
     early = shares(0)
     wait_o(0)
-    group = 6
-
-    def merge_early(k, _):
-        for r in range(group // 2):
-            wait_o(group // 2 * k + r + 1)
-        for r in range(group):
-            merge(early, group * k + r)
+    merge(early, 0)
+
+    def merge_early(t, _):
+        for c in (2 * t + 1, 2 * t + 2):
+            wait_o(c)
+        for r in range(8):
+            merge(early, 8 * t + 1 + r)
         return 0
 
-    whole = (nb - 3) // group
-    lax.fori_loop(0, whole, merge_early, 0)
-    for c in range(group // 2 * whole + 1, pairs - 1):
-        wait_o(c)
-    for b in range(group * whole, nb - 3):
+    lax.fori_loop(0, (quads - 1) // 2, merge_early, 0)
+    wait_o(quads - 1)
+    for b in range(nb - 7, nb - 3):
         merge(early, b)
     for b in (nb - 3, nb - 2):
-        wait_o(b - pairs + 2)
+        wait_o(b - nb + 3 + quads)
         merge(early, b)
     late = shares(1)
-    wait_o(pairs + 1)
+    wait_o(quads + 2)
     merge(late, nb - 1)
 
     for t in (0, 1):
@@ -266,8 +271,8 @@
             o_copy(i, c, d, peers[i]).wait_send()
         return 0
 
-    lax.fori_loop(1, pairs - 1, drain, 0)
-    for c in (0, pairs - 1, pairs, pairs + 1):
+    lax.fori_loop(1, quads, drain, 0)
+    for c in (0, quads, quads + 1, quads + 2):
         drain(c, 0)
 
     def drain_q(c, _):
@@ -315,13 +320,13 @@
                 pltpu.SemaphoreType.DMA((2,)),
                 pltpu.SemaphoreType.DMA((2, b // 2)),
                 pltpu.SemaphoreType.DMA((2, b // 2)),
-                pltpu.SemaphoreType.DMA((3, b // 2 + 2)),
-                pltpu.SemaphoreType.DMA((3, b // 2 + 2)),
+                pltpu.SemaphoreType.DMA((3, b // 4 + 3)),
+                pltpu.SemaphoreType.DMA((3, b // 4 + 3)),
                 pltpu.SemaphoreType.DMA((2, 3)),
                 pltpu.SemaphoreType.DMA((2, 3)),
             ],
             compiler_params=pltpu.CompilerParams(
-                collective_id=0, has_side_effects=True, vmem_limit_bytes=40 * 2 ** 20
+                collective_id=0, has_side_effects=True, vmem_limit_bytes=46 * 2 ** 20
             ),
             name='mla_decode',
         )(pltpu.with_memory_space_constraint(lengths, pltpu.HBM), pltpu.with_memory_space_constraint(q, pltpu.HBM), jnp.swapaxes(cache, 1, 2))

time: 47.7 us -> 48.8 us (1.023)
  Pallas kernels: 46.8 us -> 47.9 us
    pallas_call x1, Pallas kernels: 46.8 us -> 47.9 us  [local(): pl.pallas_call(kernel, out_shape=jax.ShapeDtypeStruct((b, own, lat), jnp....]
where the time goes in v6:
time: 48.8 us; the launch traced here: 48.7 us
  Pallas kernels  47.9 us (98%)
  local copies, waits for them, and re-layouts  0.8 us (2%)
    pallas_call x1, Pallas kernels, local(): pl.pallas_call(kernel, out_shape=jax.ShapeDtypeStruct((b, own, lat), jnp....  47.9 us

profile of v6, /device:TPU:0, one launch (start us, length us, event | category | flops | bytes accessed | tf_op | source)
XLA Modules:
  0.0 48.7 jit_solution(1640403859961689475)
XLA Ops:
  0.0 47.9 %mla_decode.1 = bf16[32,16,512]{2,1,0:T(8,128)(2,1)S(1)} custom-call(s32[32]{0:T(128)} %lens_ref.1, bf16[32,16,576]{2,1,0:T(8,128)(2,1)} %q_ref.1, bf16[32,576,2048]{2,1,0:T(8,128)(2,1)} %bitcast.cache_ref), custom_call_target="tpu_custom_call" | custom-call | tf_op jit(solution)/shard_map/mla_decode/pallas_call | solution.py:295
  47.9 0.8 %copy.5 = bf16[32,16,512]{2,1,0:T(8,128)(2,1)} copy(bf16[32,16,512]{2,1,0:T(8,128)(2,1)S(1)} %mla_decode.1) | data formatting | bytes 1048576

commit v7 on v5

--- a/solution.py
+++ b/solution.py
@@ -55,8 +55,8 @@
             at = pl.ds(2 * c, 2)
         return remote(obuf.at[at, rows(dst_dev), :], orecv.at[src_dev, at], os_sem.at[i, c], or_sem.at[i, c], dst_dev)
 
-    def l_copy(t, i, src_dev, dst_dev):
-        return remote(lbuf.at[t, rows(dst_dev), :], lrecv.at[t, src_dev], ls_sem.at[t, i], lr_sem.at[t, i], dst_dev)
+    def l_copy(i, src_dev, dst_dev):
+        return remote(lbuf.at[rows(dst_dev), :], lrecv.at[src_dev], ls_sem.at[i], lr_sem.at[i], dst_dev)
 
     q_own = pltpu.make_async_copy(q_ref, qbuf.at[:, rows(d), :], q_sem)
     q_own.start()
@@ -103,7 +103,7 @@
             top = t if top is None else jnp.maximum(top, t)
         return top
 
-    def weights(b, s_ref, mx_ref, src, dst):
+    def weights(b, s_ref, mx_ref):
         m = jnp.max(mx_ref[...], axis=1, keepdims=True)
         m0 = jnp.where(m == -jnp.inf, 0.0, m)
         p = jnp.exp2((s_ref[...] - m0) * (SCALE * LOG2E))
@@ -111,15 +111,17 @@
         has = l > 0.0
         l1 = jnp.where(has, l, 1.0)
         lse = jnp.where(has, m0 * SCALE + jnp.log(l1), -jnp.inf)
-        lane = lax.broadcasted_iota(jnp.int32, lbuf.shape[1:], 1)
-        lbuf[dst] = jnp.where(lane == b, lse, lbuf[src])
+        lane = lax.broadcasted_iota(jnp.int32, lbuf.shape, 1)
+        lbuf[...] = jnp.where(lane == b, lse, lbuf[...])
         return p.astype(jnp.bfloat16), 1.0 / l1
 
-    def step(bq, sq, mxq, bv, sv, mxv, dst=0, at=(0, 2, 4, 6)):
+    def step(bq, sq, mxq, bv, sv, mxv, at=(0, 2, 4, 6), known=None):
         tiles, chains = 8, 4
         w, r = sl // tiles, lat // chains
         if bv is not None:
-            pb, inv = weights(bv, sv, mxv, 0, dst)
+            pb, inv = weights(bv, sv, mxv)
+            if known is not None:
+                known()
         top = None
         acc = [None] * chains
         for j in range(tiles + 1):
@@ -137,7 +139,7 @@
         if bq is not None:
             mxq[...] = top
 
-    lbuf[0] = jnp.zeros(lbuf.shape[1:], jnp.float32)
+    lbuf[...] = jnp.zeros_like(lbuf)
     lens.wait()
     forward_q(0)
     mate_copy(1, d, mate).start()
@@ -146,11 +148,11 @@
     mate_copy(0, mate, mate).wait_recv()
     cache_copy(0).wait()
     cache_copy(1).wait()
+    wait_q(0)
+    step(0, s_a, mx_a, None, None, None)
     forward_q(1)
     cache_copy(4).start()
     cache_copy(5).start()
-    wait_q(0)
-    step(0, s_a, mx_a, None, None, None)
     step(1, s_b, mx_b, 0, s_a, mx_a)
     mate_copy(1, mate, mate).wait_recv()
 
@@ -198,24 +200,22 @@
 
     lax.fori_loop(1, pairs - 1, body, 0)
 
-    def send_l(t):
+    def send_l():
         for i in (1, 2, 0):
-            l_copy(t, i, d, peers[i]).start()
+            l_copy(i, d, peers[i]).start()
 
     enter(pairs - 1)
     first(pairs - 1)
     send_o(pairs - 1)
     second(pairs - 1)
     send_o(pairs)
-    send_l(0)
-    step(None, None, None, nb - 1, s_b, mx_b, 1)
+    step(None, None, None, nb - 1, s_b, mx_b, known=send_l)
     send_o(pairs + 1)
-    send_l(1)
-
-    def shares(t):
+
+    def shares():
         for i in (0, 1, 2):
-            l_copy(t, i, peers[i], d).wait_recv()
-        lses = [lbuf[t, rows(d), :]] + [lrecv[t, p] for p in peers]
+            l_copy(i, peers[i], d).wait_recv()
+        lses = [lbuf[rows(d), :]] + [lrecv[p] for p in peers]
         top = functools.reduce(jnp.maximum, lses)
         ws = [jnp.exp(x - top) for x in lses]
         norm = 1.0 / functools.reduce(jnp.add, ws)
@@ -231,7 +231,7 @@
             total = term if total is None else total + term
         out_ref[b] = total.astype(jnp.bfloat16)
 
-    early = shares(0)
+    early = shares()
     wait_o(0)
     group = 6
 
@@ -251,23 +251,13 @@
     for b in (nb - 3, nb - 2):
         wait_o(b - pairs + 2)
         merge(early, b)
-    late = shares(1)
-    wait_o(pairs + 1)
-    merge(late, nb - 1)
-
-    for t in (0, 1):
-        for i in (0, 1, 2):
-            l_copy(t, i, d, peers[i]).wait_send()
-    for i in (0, 1):
-        mate_copy(i, d, mate).wait_send()
-
     def drain(c, _):
         for i in (0, 1, 2):
             o_copy(i, c, d, peers[i]).wait_send()
         return 0
 
     lax.fori_loop(1, pairs - 1, drain, 0)
-    for c in (0, pairs - 1, pairs, pairs + 1):
+    for c in (0, pairs - 1, pairs):
         drain(c, 0)
 
     def drain_q(c, _):
@@ -276,6 +266,14 @@
         return 0
 
     lax.fori_loop(0, pairs, drain_q, 0)
+    for i in (0, 1):
+        mate_copy(i, d, mate).wait_send()
+    for i in (0, 1, 2):
+        l_copy(i, d, peers[i]).wait_send()
+
+    wait_o(pairs + 1)
+    merge(early, nb - 1)
+    drain(pairs + 1, 0)
 
 
 def solution(mesh):
@@ -305,8 +303,8 @@
                 pltpu.VMEM((heads, 128), jnp.float32),
                 pltpu.VMEM((b + 2, heads, lat), jnp.bfloat16),
                 pltpu.VMEM((n, b + 2, own, lat), jnp.bfloat16),
-                pltpu.VMEM((2, heads, 128), jnp.float32),
-                pltpu.VMEM((2, n, own, 128), jnp.float32),
+                pltpu.VMEM((heads, 128), jnp.float32),
+                pltpu.VMEM((n, own, 128), jnp.float32),
                 pltpu.SMEM((b,), jnp.int32),
                 pltpu.SemaphoreType.DMA,
                 pltpu.SemaphoreType.DMA((SLOTS,)),
@@ -317,8 +315,8 @@
                 pltpu.SemaphoreType.DMA((2, b // 2)),
                 pltpu.SemaphoreType.DMA((3, b // 2 + 2)),
                 pltpu.SemaphoreType.DMA((3, b // 2 + 2)),
-                pltpu.SemaphoreType.DMA((2, 3)),
-                pltpu.SemaphoreType.DMA((2, 3)),
+                pltpu.SemaphoreType.DMA((3,)),
+                pltpu.SemaphoreType.DMA((3,)),
             ],
             compiler_params=pltpu.CompilerParams(
                 collective_id=0, has_side_effects=True, vmem_limit_bytes=40 * 2 ** 20

time: 47.7 us -> 47.6 us (level)
  no operation moved by 1% of the time
where the time goes in v7:
time: 47.6 us; the launch traced here: 47.5 us
  Pallas kernels  46.6 us (98%)
  local copies, waits for them, and re-layouts  0.8 us (2%)
    pallas_call x1, Pallas kernels, local(): pl.pallas_call(kernel, out_shape=jax.ShapeDtypeStruct((b, own, lat), jnp....  46.6 us

profile of v7, /device:TPU:0, one launch (start us, length us, event | category | flops | bytes accessed | tf_op | source)
XLA Modules:
  0.0 47.5 jit_solution(15673966444785415043)
XLA Ops:
  0.0 46.6 %mla_decode.1 = bf16[32,16,512]{2,1,0:T(8,128)(2,1)S(1)} custom-call(s32[32]{0:T(128)} %lens_ref.1, bf16[32,16,576]{2,1,0:T(8,128)(2,1)} %q_ref.1, bf16[32,576,2048]{2,1,0:T(8,128)(2,1)} %bitcast.cache_ref), custom_call_target="tpu_custom_call" | custom-call | tf_op jit(solution)/shard_map/mla_decode/pallas_call | solution.py:288
  46.7 0.8 %copy.5 = bf16[32,16,512]{2,1,0:T(8,128)(2,1)} copy(bf16[32,16,512]{2,1,0:T(8,128)(2,1)S(1)} %mla_decode.1) | data formatting | bytes 1048576

commit v8 on v7

--- a/solution.py
+++ b/solution.py
@@ -10,8 +10,8 @@
 ROPE = 64
 SCALE = 192 ** -0.5
 LOG2E = 1.4426950408889634
-SLOTS = 8
-LEAD = 5
+SLOTS = 12
+LEAD = 7
 NT = (((1,), (1,)), ((), ()))
 
 
@@ -156,55 +156,96 @@
     step(1, s_b, mx_b, 0, s_a, mx_a)
     mate_copy(1, mate, mate).wait_recv()
 
-    def enter(k):
-        if not isinstance(k, int):
-            @pl.when(k < pairs - 1)
-            def _():
-                forward_q(k + 1)
-
-        wait_q(k)
-        if not isinstance(k, int):
-            @pl.when(k < pairs - LEAD + 1)
-            def _():
-                q_copy(0, k + LEAD - 1, d, over).start()
-
-            @pl.when(k < pairs - 2)
-            def _():
-                cache_copy(2 * k + 4).start()
-                cache_copy(2 * k + 5).start()
-
-            @pl.when(k == 1)
-            def _():
-                send_o(0)
-
-            @pl.when(k > 1)
-            def _():
-                send_o(k - 1)
-        else:
-            send_o(k - 1)
-
-        cache_copy(2 * k).wait()
-        cache_copy(2 * k + 1).wait()
+    def pair_starts(p):
+        cache_copy(2 * p).start()
+        cache_copy(2 * p + 1).start()
+
+    def pair_waits(p):
+        wait_q(p)
+        cache_copy(2 * p).wait()
+        cache_copy(2 * p + 1).wait()
+
+    def send_q(c):
+        q_copy(0, c, d, over).start()
+
+    inner, outer = (0, 2, 4, 6), (0, 2, 4, 8)
 
     def first(k):
-        step(2 * k, s_a, mx_a, 2 * k - 1, s_b, mx_b)
-
-    def second(k):
-        step(2 * k + 1, s_b, mx_b, 2 * k, s_a, mx_a, at=(0, 2, 4, 8))
-
-    def body(k, _):
-        enter(k)
+        step(2 * k, s_a, mx_a, 2 * k - 1, s_b, mx_b, at=inner)
+
+    def second(k, at=outer):
+        step(2 * k + 1, s_b, mx_b, 2 * k, s_a, mx_a, at=at)
+
+    def opening(k, _):
+        forward_q(k + 1)
+        send_q(k + LEAD - 1)
+
+        @pl.when(k == 1)
+        def _():
+            send_o(0)
+
+        @pl.when(k == 2)
+        def _():
+            forward_q(4)
+            send_q(LEAD + 2)
+            send_o(1)
+
+        pair_starts(k + 2)
+        pair_waits(k)
         first(k)
         second(k)
         return 0
 
-    lax.fori_loop(1, pairs - 1, body, 0)
+    lax.fori_loop(1, 3, opening, 0)
+
+    def middle(t, _):
+        k = 2 * t + 1
+        forward_q(k + 2)
+        forward_q(k + 3)
+
+        @pl.when(k + LEAD + 1 < pairs)
+        def _():
+            send_q(k + LEAD)
+            send_q(k + LEAD + 1)
+
+        @pl.when(t > 1)
+        def _():
+            send_o(k - 2)
+
+        send_o(k - 1)
+        pair_starts(k + 2)
+        pair_starts(k + 3)
+        pair_waits(k)
+        pair_waits(k + 1)
+        first(k)
+        second(k, inner)
+        first(k + 1)
+        second(k + 1)
+        return 0
+
+    lax.fori_loop(1, pairs // 2 - 2, middle, 0)
+
+    def closing(k, _):
+        @pl.when(k == pairs - 3)
+        def _():
+            forward_q(pairs - 1)
+            pair_starts(pairs - 1)
+            send_o(pairs - 5)
+
+        send_o(k - 1)
+        pair_waits(k)
+        first(k)
+        second(k)
+        return 0
+
+    lax.fori_loop(pairs - 3, pairs - 1, closing, 0)
 
     def send_l():
         for i in (1, 2, 0):
             l_copy(i, d, peers[i]).start()
 
-    enter(pairs - 1)
+    send_o(pairs - 2)
+    pair_waits(pairs - 1)
     first(pairs - 1)
     send_o(pairs - 1)
     second(pairs - 1)
@@ -319,7 +360,7 @@
                 pltpu.SemaphoreType.DMA((3,)),
             ],
             compiler_params=pltpu.CompilerParams(
-                collective_id=0, has_side_effects=True, vmem_limit_bytes=40 * 2 ** 20
+                collective_id=0, has_side_effects=True, vmem_limit_bytes=46 * 2 ** 20
             ),
             name='mla_decode',
         )(pltpu.with_memory_space_constraint(lengths, pltpu.HBM), pltpu.with_memory_space_constraint(q, pltpu.HBM), jnp.swapaxes(cache, 1, 2))

time: 47.6 us -> 47 us (0.987)
  Pallas kernels: 46.6 us -> 46.1 us
    pallas_call x1, Pallas kernels: 46.6 us -> 46.1 us  [local(): pl.pallas_call(kernel, out_shape=jax.ShapeDtypeStruct((b, own, lat), jnp....]
where the time goes in v8:
time: 47 us; the launch traced here: 46.9 us
  Pallas kernels  46.1 us (98%)
  local copies, waits for them, and re-layouts  0.8 us (2%)
    pallas_call x1, Pallas kernels, local(): pl.pallas_call(kernel, out_shape=jax.ShapeDtypeStruct((b, own, lat), jnp....  46.1 us

profile of v8, /device:TPU:0, one launch (start us, length us, event | category | flops | bytes accessed | tf_op | source)
XLA Modules:
  0.0 46.9 jit_solution(1524959159497609470)
XLA Ops:
  0.0 46.1 %mla_decode.1 = bf16[32,16,512]{2,1,0:T(8,128)(2,1)S(1)} custom-call(s32[32]{0:T(128)} %lens_ref.1, bf16[32,16,576]{2,1,0:T(8,128)(2,1)} %q_ref.1, bf16[32,576,2048]{2,1,0:T(8,128)(2,1)} %bitcast.cache_ref), custom_call_target="tpu_custom_call" | custom-call | tf_op jit(solution)/shard_map/mla_decode/pallas_call | solution.py:329
  46.1 0.8 %copy.5 = bf16[32,16,512]{2,1,0:T(8,128)(2,1)} copy(bf16[32,16,512]{2,1,0:T(8,128)(2,1)S(1)} %mla_decode.1) | data formatting | bytes 1048576

commit v9 on v8

--- a/solution.py
+++ b/solution.py
@@ -45,7 +45,11 @@
         return remote(view, view, ms_sem.at[i], mr_sem.at[i], to)
 
     def q_copy(kind, c, src_dev, to):
-        view = qbuf.at[pl.ds(2 * c, 2), rows(src_dev), :]
+        if isinstance(c, int) and c in (0, pairs):
+            at = pl.ds(0 if c == 0 else 1, 1)
+        else:
+            at = pl.ds(2 * c, 2)
+        view = qbuf.at[at, rows(src_dev), :]
         return remote(view, view, qs_sem.at[kind, c], qr_sem.at[kind, c], to)
 
     def o_copy(i, c, src_dev, dst_dev):
@@ -58,8 +62,10 @@
     def l_copy(i, src_dev, dst_dev):
         return remote(lbuf.at[rows(dst_dev), :], lrecv.at[src_dev], ls_sem.at[i], lr_sem.at[i], dst_dev)
 
-    q_own = pltpu.make_async_copy(q_ref, qbuf.at[:, rows(d), :], q_sem)
-    q_own.start()
+    q_own = [pltpu.make_async_copy(q_ref.at[at], qbuf.at[at, rows(d), :], q_sem.at[i])
+             for i, at in enumerate((pl.ds(0, 2), pl.ds(2, nb - 2)))]
+    for copy in q_own:
+        copy.start()
     lens = pltpu.make_async_copy(lens_ref, len_ref, n_sem)
     lens.start()
 
@@ -68,10 +74,12 @@
         pl.semaphore_signal(barrier, inc=1, device_id=(g, p), device_id_type=pl.DeviceIdType.MESH)
     pl.semaphore_wait(barrier, 3)
 
-    q_own.wait()
+    q_own[0].wait()
     q_copy(0, 0, d, over).start()
+    q_copy(0, pairs, d, over).start()
     mate_copy(0, d, mate).start()
     cache_copy(0).start()
+    q_own[1].wait()
     for c in range(1, LEAD):
         q_copy(0, c, d, over).start()
     cache_copy(1).start()
@@ -142,6 +150,7 @@
     lbuf[...] = jnp.zeros_like(lbuf)
     lens.wait()
     forward_q(0)
+    forward_q(pairs)
     mate_copy(1, d, mate).start()
     cache_copy(2).start()
     cache_copy(3).start()
@@ -150,6 +159,7 @@
     cache_copy(1).wait()
     wait_q(0)
     step(0, s_a, mx_a, None, None, None)
+    wait_q(pairs)
     forward_q(1)
     cache_copy(4).start()
     cache_copy(5).start()
@@ -306,7 +316,9 @@
         q_copy(1, c, over, mate).wait_send()
         return 0
 
-    lax.fori_loop(0, pairs, drain_q, 0)
+    lax.fori_loop(1, pairs, drain_q, 0)
+    for c in (0, pairs):
+        drain_q(c, 0)
     for i in (0, 1):
         mate_copy(i, d, mate).wait_send()
     for i in (0, 1, 2):
@@ -349,11 +361,11 @@
                 pltpu.SMEM((b,), jnp.int32),
                 pltpu.SemaphoreType.DMA,
                 pltpu.SemaphoreType.DMA((SLOTS,)),
-                pltpu.SemaphoreType.DMA,
                 pltpu.SemaphoreType.DMA((2,)),
                 pltpu.SemaphoreType.DMA((2,)),
-                pltpu.SemaphoreType.DMA((2, b // 2)),
-                pltpu.SemaphoreType.DMA((2, b // 2)),
+                pltpu.SemaphoreType.DMA((2,)),
+                pltpu.SemaphoreType.DMA((2, b // 2 + 1)),
+                pltpu.SemaphoreType.DMA((2, b // 2 + 1)),
                 pltpu.SemaphoreType.DMA((3, b // 2 + 2)),
                 pltpu.SemaphoreType.DMA((3, b // 2 + 2)),
                 pltpu.SemaphoreType.DMA((3,)),

time: 47 us -> 46.7 us (level)
  no operation moved by 1% of the time
where the time goes in v9:
time: 46.7 us; the launch traced here: 46.5 us
  Pallas kernels  45.7 us (98%)
  local copies, waits for them, and re-layouts  0.8 us (2%)
    pallas_call x1, Pallas kernels, local(): pl.pallas_call(kernel, out_shape=jax.ShapeDtypeStruct((b, own, lat), jnp....  45.7 us

profile of v9, /device:TPU:0, one launch (start us, length us, event | category | flops | bytes accessed | tf_op | source)
XLA Modules:
  0.0 46.5 jit_solution(1491721793127628666)
XLA Ops:
  0.0 45.7 %mla_decode.1 = bf16[32,16,512]{2,1,0:T(8,128)(2,1)S(1)} custom-call(s32[32]{0:T(128)} %lens_ref.1, bf16[32,16,576]{2,1,0:T(8,128)(2,1)} %q_ref.1, bf16[32,576,2048]{2,1,0:T(8,128)(2,1)} %bitcast.cache_ref), custom_call_target="tpu_custom_call" | custom-call | tf_op jit(solution)/shard_map/mla_decode/pallas_call | solution.py:341
  45.8 0.8 %copy.5 = bf16[32,16,512]{2,1,0:T(8,128)(2,1)} copy(bf16[32,16,512]{2,1,0:T(8,128)(2,1)S(1)} %mla_decode.1) | data formatting | bytes 1048576
